TPU v7x, 32 devices: a whole 2x2x4 slice. The times are simulated.
32 devices in a mesh: groups: 2 (over y), dp: 4 (over z), layer: 4 (over x, core).
Axes of the slice: x: 2, y: 2, z: 4, core: 2. Of those that a mesh axis runs over, the one named last changes fastest.
Arguments:
- layer_inputs: float32 [4, 1024, 512], P('layer', ('groups', 'dp')), parts along dimension 1, may hold values from -6 to 6
- pre_acts: float32 [4, 1024, 512], P('layer', ('groups', 'dp')), parts along dimension 1, may hold values from -6 to 6
- layer_outputs: float32 [4, 1024, 512], P('layer', ('groups', 'dp')), parts along dimension 1, may hold values from -6 to 6
- multipliers: float32 [4, 1024, 512], P('layer', ('groups', 'dp')), parts along dimension 1, may hold values from -6 to 6
- weights: float32 [8, 512, 512], P(('groups', 'layer')), parts along dimension 0, may hold values from -0.25 to 0.25
- biases: float32 [8, 512], P(('groups', 'layer')), parts along dimension 0, may hold values from -3 to 3
- prev_outputs: float32 [1024, 512], P(('groups', 'dp')), parts along dimension 0, may hold values from -6 to 6
- prev_multipliers: float32 [1024, 512], P(('groups', 'dp')), parts along dimension 0, may hold values from -6 to 6
- next_inputs: float32 [1024, 512], P(('groups', 'dp')), parts along dimension 0, may hold values from -6 to 6
- row_order: int32 [8, 128], P(('groups', 'dp')), parts along dimension 0, may hold values from 0 to 127, each once within a row
Outputs:
- new_inputs: float32 [4, 1024, 512], P('layer', ('groups', 'dp')), parts along dimension 1
- new_preacts: float32 [4, 1024, 512], P('layer', ('groups', 'dp')), parts along dimension 1
- new_outputs: float32 [4, 1024, 512], P('layer', ('groups', 'dp')), parts along dimension 1
- new_multipliers: float32 [4, 1024, 512], P('layer', ('groups', 'dp')), parts along dimension 1
- new_weights: float32 [8, 512, 512], P(('groups', 'layer')), parts along dimension 0
- new_biases: float32 [8, 512], P(('groups', 'layer')), parts along dimension 0
There are 2 independent parts, one for each index of `groups`. A program takes and returns all parts, laid end to end along the dimension named above; each array names one. Nothing has to cross between parts.
Inputs may be any that keep to these rules, and one draw needn't show every extreme that they name: Each row of row_order holds every number of 0 to 127 once.
All inputs are finite; a program needn't handle non-finite values.
Results may differ from a plain program's by a relative error of at most 0.0001.
Values sent between devices are 32-bit elements; how exact they have to be, the bound alone decides.
No kernel may reach another device: no remote copies, remote signals or barrier semaphores. Data moves between devices by JAX's collectives and lax.ppermute only.
A program may use at most 64 MiB of HBM per device.

v0:
```python
import jax
import jax.numpy as jnp
from jax import lax
from jax.experimental import pallas as pl
from jax.experimental.pallas import tpu as pltpu
from jax.sharding import PartitionSpec as P


INNER = 3


penalty_nu = 1.0
penalty_rho = 1.0
step_input = 0.2
step_weight = 0.3
step_preact = 0.5


def from_behind(x, axis, by):
    count = lax.axis_size(axis)
    pairs = [(i, i + by) for i in range(count) if 0 <= i + by < count]
    return lax.ppermute(x, axis, pairs)


def matmul(left, right):
    return jnp.dot(left, right, precision=lax.Precision.HIGHEST)


def line_plan(count):
    outbox = {(i, side): [i] for i in range(count) for side in (-1, 1)}
    rounds = []
    while any(outbox[i, side] for i in range(count) for side in (-1, 1) if 0 <= i + side < count):
        for parity in (0, 1):
            sends = []
            for i in range(count):
                side = 1 if i % 2 == parity else -1
                if 0 <= i + side < count and outbox[i, side]:
                    sends.append((i, i + side, outbox[i, side].pop(0)))
            for source, target, block in sends:
                outbox[target, target - source].append(block)
            if sends:
                rounds.append(sends)
    return rounds


def gather_line(own, axis):
    count = lax.axis_size(axis)
    me = lax.axis_index(axis)
    held = {(i, i): own for i in range(count)}
    slots = [[] for _ in range(count - 1)]
    got = [0] * count
    for sends in line_plan(count):
        by_value = {}
        for source, target, block in sends:
            value = held[source, block]
            by_value.setdefault(id(value), (value, []))[1].append(source)
        (payload, _), *others = by_value.values()
        for value, sources in others:
            mine = jnp.any(jnp.asarray(sources) == me)
            payload = jnp.where(mine, value, payload)
        arrived = lax.ppermute(payload, axis, [(s, t) for s, t, _ in sends])
        filled = []
        for source, target, block in sends:
            held[target, block] = arrived
            if got[target] not in filled:
                filled.append(got[target])
            got[target] += 1
        for slot in filled:
            slots[slot].append(arrived)
    return slots


def summed_steps(inputs, preact, weight, offset, scale):
    row_count = inputs.shape[0] * lax.axis_size("dp")
    gram_matrix, cross_term, column_sums, preact_sums = lax.psum(
        (
            matmul(inputs.T, inputs),
            matmul(inputs.T, preact),
            jnp.sum(inputs, axis=0),
            jnp.sum(preact, axis=0),
        ),
        "dp",
    )
    for _ in range(INNER):
        grad_weight = (
            matmul(gram_matrix, weight) + column_sums[:, None] * offset[None, :] - cross_term
        )
        grad_offset = matmul(column_sums[None, :], weight)[0] + row_count * offset - preact_sums
        weight = weight - scale * grad_weight
        offset = offset - scale * grad_offset
    return weight, offset


VMEM = pl.BlockSpec(memory_space=pltpu.VMEM)
HBM = pl.BlockSpec(memory_space=pltpu.HBM)
NN = (((1,), (0,)), ((), ()))
NT = (((1,), (1,)), ((), ()))


def f32(*shape):
    return jax.ShapeDtypeStruct(shape, jnp.float32)


def bf16(*shape):
    return jax.ShapeDtypeStruct(shape, jnp.bfloat16)


def run(kernel, args, outs, flops, out_specs=None, scratch=()):
    nbytes = sum(x.size * x.dtype.itemsize for x in (*args, *outs))
    return pl.pallas_call(
        kernel,
        out_shape=outs,
        in_specs=[VMEM] * len(args),
        out_specs=[VMEM] * len(outs) if out_specs is None else out_specs,
        scratch_shapes=scratch,
        cost_estimate=pl.CostEstimate(flops=flops, bytes_accessed=nbytes, transcendentals=0),
        compiler_params=pltpu.CompilerParams(vmem_limit_bytes=24 * 2**20),
    )(*args)


def split(x):
    high = x.astype(jnp.bfloat16)
    return high, (x - high.astype(jnp.float32)).astype(jnp.bfloat16)


def dot3(left, right, dims=NN):
    one = lambda a, b: lax.dot_general(a, b, dims, preferred_element_type=jnp.float32)
    return one(left[0], right[0]) + (one(left[0], right[1]) + one(left[1], right[0]))


def pick_rows(rows, order):
    count = rows.shape[0]
    hot = (lax.broadcasted_iota(jnp.int32, (count, count), 0) == order).astype(jnp.float32)
    hot = hot.T.astype(jnp.bfloat16)
    high, low = split(rows)
    rest = (rows - high.astype(jnp.float32) - low.astype(jnp.float32)).astype(jnp.bfloat16)
    one = lambda b: lax.dot_general(hot, b, NN, preferred_element_type=jnp.float32)
    return one(high) + (one(low) + one(rest))


def softplus(v):
    return jnp.maximum(v, 0.0) + jnp.log1p(jnp.exp(-jnp.abs(v)))


def minus_kernel(u, q, out):
    out[...] = u[0] - penalty_rho * q[0]


def input_kernel(p, z, w, b, qb, ub, order, out):
    weight = split(w[0])
    residual = dot3(split(p[0]), weight) + b[...] - z[0]
    step = penalty_nu * dot3(split(residual), weight, NT) + penalty_rho * p[0]
    out[...] = p[0] - step_input * step

    @pl.when(lax.axis_index("layer") == 0)
    def _():
        out[...] -= step_input * pick_rows(ub[...] - penalty_rho * qb[...], order[...])


def total_of(refs):
    value = refs[0][...]
    for ref in refs[1:]:
        value = value + ref[...]
    return value


def gathered_pass(inputs, preact, outputs, duals, weight, offset, after_in, next_inputs, row_order, p_slots, z_slots, scale):
    rows, width = inputs.shape
    early_count = rows * len(p_slots)
    count = early_count + rows
    p_early = [[inputs]] + p_slots[:-1]
    z_early = [[preact[0]]] + z_slots[:-1]
    p_late, z_late = p_slots[-1], z_slots[-1]
    sizes = [len(parts) for parts in p_early]
    unit = 2 * rows * width * width * 3

    def group(refs, counts):
        out = []
        for n in counts:
            out.append(refs[:n])
            refs = refs[n:]
        return out

    def early_kernel(*refs):
        ins = refs[: 2 * sum(sizes)]
        w, b, z, q, u, pn, pb, order = refs[2 * sum(sizes) : 2 * sum(sizes) + 8]
        residual, kernel, z_part, q_part = refs[2 * sum(sizes) + 8 :]
        p_refs, z_refs = group(ins[: sum(sizes)], sizes), group(ins[sum(sizes) :], sizes)
        wide = split(w[0])
        blocks = [split(total_of(r)) for r in p_refs]
        for i, block in enumerate(blocks):
            at = slice(i * rows, (i + 1) * rows)
            residual[at] = dot3(block, wide) + b[...] - total_of(z_refs[i])
            for j in range(i + 1):
                to = slice(j * rows, (j + 1) * rows)
                piece = scale * (dot3(block, blocks[j], NT) + 1.0)
                kernel[at, to] = piece
                if j < i:
                    kernel[to, at] = piece.T
        value = z[0]
        z_part[...] = (1 - step_preact) * value - step_preact * (
            (softplus(value) - q[0]) * jax.nn.sigmoid(value)
        )
        q_part[...] = u[0] + penalty_rho * pn[...]

        @pl.when(lax.axis_index("layer") == lax.axis_size("layer") - 1)
        def _():
            q_part[...] += penalty_rho * pick_rows(pb[...], order[...])

    args = [x for parts in p_early for x in parts] + [x for parts in z_early for x in parts]
    args += [weight, offset, preact, outputs, duals, after_in, next_inputs, row_order]
    residual, kernel, z_part, q_part = run(
        early_kernel,
        args,
        [f32(early_count, width), f32(early_count, early_count), f32(rows, width), f32(rows, width)],
        unit * (2 * len(sizes)),
    )

    def solve_kernel(*refs):
        ins = refs[: sum(sizes) + len(p_late)]
        residual, kernel, w, b = refs[len(ins) : len(ins) + 4]
        w_part, b_part, pull_high, pull_low, weigh, a_part, a_pull = refs[len(ins) + 4 : len(ins) + 11]
        j_ref, turned = refs[len(ins) + 11 :]
        wide = split(w[0])
        every = [total_of(r) for r in group(ins, sizes + [len(p_late)])]
        late = split(every[-1])
        j_ref[:early_count, :early_count] = kernel[...]
        for i, block in enumerate(every):
            at = slice(i * rows, (i + 1) * rows)
            turned[:, at] = block.T
            piece = scale * (dot3(split(block), late, NT) + 1.0)
            j_ref[at, early_count:] = piece
            if i * rows < early_count:
                j_ref[early_count:, at] = piece.T
        j = j_ref[...]
        both = split(j)
        eye = (
            lax.broadcasted_iota(jnp.int32, (count, count), 0)
            == lax.broadcasted_iota(jnp.int32, (count, count), 1)
        ).astype(jnp.float32)
        total = eye
        for inner_step in range(1, INNER):
            total = eye + total - (dot3(both, split(total)) if inner_step > 1 else j)
        pull = scale * dot3(split(turned[...]), split(total))
        sums = scale * jnp.sum(total, axis=1, keepdims=True)
        start = jnp.concatenate([residual[...], dot3(late, wide) + b[...]], axis=0)
        new = w[0] - dot3(split(pull), split(start))
        w_part[...] = new
        new_b = b[...] - jnp.sum(sums * start, axis=0, keepdims=True)
        b_part[...] = new_b
        pull_high[...], pull_low[...] = split(pull[:, early_count:])
        weigh[...] = jnp.broadcast_to(sums[early_count:], weigh.shape)
        own = split(every[0])
        a_part[...] = dot3(own, split(new)) + new_b
        a_pull[...] = dot3(own, (pull_high[...], pull_low[...]))

    args = [x for parts in p_early + [p_late] for x in parts] + [residual, kernel, weight, offset]
    solved = run(
        solve_kernel,
        args,
        [
            f32(width, width),
            f32(1, width),
            bf16(width, rows),
            bf16(width, rows),
            f32(rows, 128),
            f32(rows, width),
            f32(rows, rows),
        ],
        unit * (3 * len(p_slots) + 4),
        scratch=[pltpu.VMEM((count, count), jnp.float32), pltpu.VMEM((width, count), jnp.float32)],
    )

    def last_kernel(*refs):
        late_refs = refs[: len(z_late)]
        w_part, b_part, pull_high, pull_low, weigh, a_part, a_pull, z_part, q_part = refs[
            len(z_late) : len(z_late) + 9
        ]
        z_out, q_out, u_out, w_out, b_out = refs[len(z_late) + 9 : len(z_late) + 14]
        z_own, q_own, u_own, w_own, b_own, sems = refs[len(z_late) + 14 :]
        value = total_of(late_refs)
        late = split(value)
        new_w = w_part[...] + dot3((pull_high[...], pull_low[...]), late)
        w_own[0] = new_w
        copies = [pltpu.make_async_copy(w_own, w_out, sems.at[0])]
        copies[-1].start()
        shift = jnp.sum(weigh[:, :1] * value, axis=0, keepdims=True)
        b_own[...] = b_part[...] + shift
        copies.append(pltpu.make_async_copy(b_own, b_out, sems.at[1]))
        copies[-1].start()
        target = a_part[...] + shift + dot3(split(a_pull[...]), late)
        new_z = z_part[...] + step_preact * target
        z_own[0] = new_z
        copies.append(pltpu.make_async_copy(z_own, z_out, sems.at[2]))
        copies[-1].start()
        both = q_part[...]
        new_q = (penalty_nu * softplus(new_z) + both) / (penalty_nu + penalty_rho)
        q_own[0] = new_q
        copies.append(pltpu.make_async_copy(q_own, q_out, sems.at[3]))
        copies[-1].start()
        u_own[0] = both - penalty_rho * new_q
        copies.append(pltpu.make_async_copy(u_own, u_out, sems.at[4]))
        copies[-1].start()
        for copy in copies:
            copy.wait()

    one = f32(1, rows, width)
    outs = [one, one, one, f32(1, width, width), f32(1, width)]
    return run(
        last_kernel,
        list(z_late) + list(solved) + [z_part, q_part],
        outs,
        unit * 2,
        out_specs=[HBM] * len(outs),
        scratch=[pltpu.VMEM(o.shape, jnp.float32) for o in outs] + [pltpu.SemaphoreType.DMA((5,))],
    )


def gathered_body(
    layer_inputs, pre_acts, layer_outputs, multipliers, weights, biases,
    prev_outputs, prev_multipliers, next_inputs, row_order,
):
    rows, width = layer_inputs.shape[1:]
    scale = step_weight / (rows * lax.axis_size("dp"))
    unit = 2 * rows * width * width * 3
    z_slots = gather_line(pre_acts[0], "dp")
    (before,) = run(minus_kernel, (multipliers, layer_outputs), [f32(rows, width)], unit // 10)
    before = from_behind(before, "layer", 1)
    (inputs,) = run(
        input_kernel,
        (layer_inputs, pre_acts, weights, biases, prev_outputs, prev_multipliers, row_order),
        [f32(rows, width)],
        unit * 2,
    )
    inputs = inputs - step_input * before
    p_slots = gather_line(inputs, "dp")
    after_in = from_behind(inputs, "layer", -1)
    z, q, u, w, b = gathered_pass(
        inputs, pre_acts, layer_outputs, multipliers, weights, biases,
        after_in, next_inputs, row_order, p_slots, z_slots, scale,
    )
    return (inputs[None], z, q, u, w, b)


def summed_body(
    layer_inputs,
    pre_acts,
    layer_outputs,
    multipliers,
    weights,
    biases,
    prev_outputs,
    prev_multipliers,
    next_inputs,
    row_order,
):
    row_perm = row_order[0]
    first_layer = lax.axis_index("layer") == 0
    last_layer = lax.axis_index("layer") == lax.axis_size("layer") - 1
    inputs, preact, outputs, duals = (
        layer_inputs[0],
        pre_acts[0],
        layer_outputs[0],
        multipliers[0],
    )
    weight, offset = (weights[0], biases[0])
    row_count = inputs.shape[0] * lax.axis_size("dp")
    scale = step_weight / row_count
    before = from_behind(duals - penalty_rho * outputs, "layer", 1)
    edge_before = jnp.take(prev_multipliers - penalty_rho * prev_outputs, row_perm, axis=0)
    before = jnp.where(first_layer, edge_before, before)
    residual = matmul(inputs, weight) + offset[None, :] - preact
    inputs = inputs - step_input * (
        penalty_nu * matmul(residual, weight.T) + penalty_rho * inputs + before
    )
    after_in = from_behind(inputs, "layer", -1)
    weight, offset = summed_steps(inputs, preact, weight, offset, scale)
    target = matmul(inputs, weight) + offset[None, :]
    preact = preact - step_preact * (
        preact - target + (jax.nn.softplus(preact) - outputs) * jax.nn.sigmoid(preact)
    )
    edge_inputs = jnp.take(next_inputs, row_perm, axis=0)
    after_in = jnp.where(last_layer, edge_inputs, after_in)
    outputs = (penalty_nu * jax.nn.softplus(preact) + duals + penalty_rho * after_in) / (
        penalty_nu + penalty_rho
    )
    duals = duals + penalty_rho * (after_in - outputs)
    return (inputs[None], preact[None], outputs[None], duals[None], weight[None], offset[None])


def body(*args):
    inputs = args[0]
    count = lax.axis_size("dp")
    gathers = 1 < count and inputs.shape[1] * count <= 2 * inputs.shape[2]
    return (gathered_body if gathers else summed_body)(*args)


def solution(mesh):
    return jax.shard_map(
        body,
        mesh=mesh,
        in_specs=(
            P("layer", ("groups", "dp"), None),
            P("layer", ("groups", "dp"), None),
            P("layer", ("groups", "dp"), None),
            P("layer", ("groups", "dp"), None),
            P(("groups", "layer"), None, None),
            P(("groups", "layer"), None),
            P(("groups", "dp"), None),
            P(("groups", "dp"), None),
            P(("groups", "dp"), None),
            P(("groups", "dp"), None),
        ),
        out_specs=(
            P("layer", ("groups", "dp"), None),
            P("layer", ("groups", "dp"), None),
            P("layer", ("groups", "dp"), None),
            P("layer", ("groups", "dp"), None),
            P(("groups", "layer"), None, None),
            P(("groups", "layer"), None),
        ),
        check_vma=False,
    )
```

profile of v0, /device:TPU:0, one launch (start us, length us, event | category | flops | bytes accessed | tf_op | source)
XLA Modules:
  0.0 57.1 jit_solution(10960927541547562251)
XLA Ops:
  0.7 1.0 %copy-done.6 = f32[1,128,512]{2,1,0:T(8,128)S(1)} copy-done((f32[1,128,512]{2,1,0:T(8,128)S(1)}, f32[1,128,512]{2,1,0:T(8,128)}, u32[]{:S(2)}) %copy-start.6) | copy-done | bytes 262168
  1.7 0.9 %copy-done.8 = f32[1,128,512]{2,1,0:T(8,128)S(1)} copy-done((f32[1,128,512]{2,1,0:T(8,128)S(1)}, f32[1,128,512]{2,1,0:T(8,128)}, u32[]{:S(2)}) %copy-start.8) | copy-done | bytes 262168
  2.7 2.4 %collective-permute-start = (f32[128,512]{1,0:T(8,128)S(1)}, f32[128,512]{1,0:T(8,128)S(1)}, u32[]{:S(2)}, u32[]{:S(2)}) collective-permute-start(f32[128,512]{1,0:T(8,128)S(1)} %shard_map.146), channel_id=1, source_target_pairs={{0,1},{1,2},{2,3},{4,5},{5,6},{6,7},{8,9},{9,10},{10,11},{12,13},{... | collective-permute-start | bytes 786440 | tf_op jit(solution)/shard_map/ppermute | solution.py:22
  5.1 1.2 %copy-done = f32[1,512,512]{2,1,0:T(8,128)S(1)} copy-done((f32[1,512,512]{2,1,0:T(8,128)S(1)}, f32[1,512,512]{2,1,0:T(8,128)}, u32[]{:S(2)}) %copy-start) | copy-done | bytes 1048600
  6.3 0.9 %copy-done.5 = f32[1,128,512]{2,1,0:T(8,128)S(1)} copy-done((f32[1,128,512]{2,1,0:T(8,128)S(1)}, f32[1,128,512]{2,1,0:T(8,128)}, u32[]{:S(2)}) %copy-start.5) | copy-done | bytes 262168
  7.3 0.7 %copy-done.10 = f32[1,512]{1,0:T(1,128)S(1)} copy-done((f32[1,512]{1,0:T(1,128)S(1)}, f32[1,512]{1,0:T(1,128)}, u32[]{:S(2)}) %copy-start.10) | copy-done | bytes 2072
  8.6 1.3 %shard_map.145 = f32[128,512]{1,0:T(8,128)S(1)} custom-call(f32[1,128,512]{2,1,0:T(8,128)S(1)} %copy-done.2, f32[1,128,512]{2,1,0:T(8,128)S(1)} %copy-done.5, f32[1,512,512]{2,1,0:T(8,128)S(1)} %copy-done, f32[1,512]{1,0:T(1,128)S(1)} %copy-done.10, f32[128,512]{1,0:T(8,128)S(1)} %copy-done.3, f32[128,512]{1,0:T(8,128)S(1)} %copy-done.4, s32[1,128]{1,0:T(1,128)S(1)} %copy-done.12), custom_call_target="tpu_custom_call" | custom-call | flops 402653184 | bytes 2361856 | tf_op jit(solution)/shard_map/pallas_call | solution.py:110
  10.0 2.5 %collective-permute-start.4 = (f32[128,512]{1,0:T(8,128)S(1)}, f32[128,512]{1,0:T(8,128)S(1)}, u32[]{:S(2)}, u32[]{:S(2)}) collective-permute-start(f32[128,512]{1,0:T(8,128)S(1)} %multiply_subtract_fusion.refs_0_), channel_id=1, source_target_pairs={{0,4},{4,0},{8,12},{12,8},{1,5},{5,1},{9,13},{13,9},{2,6},{6,2},{1... | collective-permute-start | bytes 786440 | tf_op jit(solution)/shard_map/ppermute | solution.py:61
  13.2 0.7 %collective-permute-start.5 = (f32[128,512]{1,0:T(8,128)S(1)}, f32[128,512]{1,0:T(8,128)S(1)}, u32[]{:S(2)}, u32[]{:S(2)}) collective-permute-start(f32[128,512]{1,0:T(8,128)S(1)} %multiply_subtract_fusion.refs_0_), channel_id=1, source_target_pairs={{4,8},{8,4},{5,9},{9,5},{6,10},{10,6},{7,11},{11,7},{20,24},{24,20... | collective-permute-start | bytes 786440 | tf_op jit(solution)/shard_map/ppermute | solution.py:61
  13.9 4.8 %collective-permute-done.4.refs_1_ = f32[128,512]{1,0:T(8,128)S(1)} collective-permute-done((f32[128,512]{1,0:T(8,128)S(1)}, f32[128,512]{1,0:T(8,128)S(1)}, u32[]{:S(2)}, u32[]{:S(2)}) %collective-permute-start.4) | collective-permute-done | bytes 262176 | tf_op jit(solution)/shard_map/ppermute | solution.py:61
  19.4 1.3 %collective-permute-start.11 = (f32[128,512]{1,0:T(8,128)S(1)}, f32[128,512]{1,0:T(8,128)S(1)}, u32[]{:S(2)}, u32[]{:S(2)}) collective-permute-start(f32[128,512]{1,0:T(8,128)S(1)} %multiply_subtract_fusion.refs_0_), channel_id=1, source_target_pairs={{1,0},{2,1},{3,2},{5,4},{6,5},{7,6},{9,8},{10,9},{11,10},{13,12},{... | collective-permute-start | bytes 786440 | tf_op jit(solution)/shard_map/ppermute | solution.py:22
  20.7 3.6 %collective-permute-done.1.refs_5_ = f32[128,512]{1,0:T(8,128)S(1)} collective-permute-done((f32[128,512]{1,0:T(8,128)S(1)}, f32[128,512]{1,0:T(8,128)S(1)}, u32[]{:S(2)}, u32[]{:S(2)}) %collective-permute-start.1) | collective-permute-done | bytes 262176 | tf_op jit(solution)/shard_map/ppermute | solution.py:61
  24.3 0.7 %collective-permute-start.2 = (f32[128,512]{1,0:T(8,128)S(1)}, f32[128,512]{1,0:T(8,128)S(1)}, u32[]{:S(2)}, u32[]{:S(2)}) collective-permute-start(f32[128,512]{1,0:T(8,128)S(1)} %collective-permute-done.1.refs_5_), channel_id=1, source_target_pairs={{4,8},{8,4},{5,9},{9,5},{6,10},{10,6},{7,11},{11,7},{20,24},{24,20... | collective-permute-start | bytes 786440 | tf_op jit(solution)/shard_map/ppermute | solution.py:61
  25.0 1.3 %collective-permute-start.10 = (f32[128,512]{1,0:T(8,128)S(1)}, f32[128,512]{1,0:T(8,128)S(1)}, u32[]{:S(2)}, u32[]{:S(2)}) collective-permute-start(f32[128,512]{1,0:T(8,128)S(1)} %collective-permute-done.9.refs_6_), channel_id=1, source_target_pairs={{4,0},{8,12},{5,1},{9,13},{6,2},{10,14},{7,3},{11,15},{20,16},{24,... | collective-permute-start | bytes 786440 | tf_op jit(solution)/shard_map/ppermute | solution.py:61
  26.3 1.3 %collective-permute-start.6 = (f32[128,512]{1,0:T(8,128)S(1)}, f32[128,512]{1,0:T(8,128)S(1)}, u32[]{:S(2)}, u32[]{:S(2)}) collective-permute-start(f32[128,512]{1,0:T(8,128)S(1)} %collective-permute-done.5.refs_2_), channel_id=1, source_target_pairs={{4,0},{8,12},{5,1},{9,13},{6,2},{10,14},{7,3},{11,15},{20,16},{24,... | collective-permute-start | bytes 786440 | tf_op jit(solution)/shard_map/ppermute | solution.py:61
  27.6 1.3 %collective-permute-start.8 = (f32[128,512]{1,0:T(8,128)S(1)}, f32[128,512]{1,0:T(8,128)S(1)}, u32[]{:S(2)}, u32[]{:S(2)}) collective-permute-start(f32[128,512]{1,0:T(8,128)S(1)} %collective-permute-done.7.refs_4_), channel_id=1, source_target_pairs={{4,0},{8,12},{5,1},{9,13},{6,2},{10,14},{7,3},{11,15},{20,16},{24,... | collective-permute-start | bytes 786440 | tf_op jit(solution)/shard_map/ppermute | solution.py:61
  29.0 1.3 %collective-permute-start.3 = (f32[128,512]{1,0:T(8,128)S(1)}, f32[128,512]{1,0:T(8,128)S(1)}, u32[]{:S(2)}, u32[]{:S(2)}) collective-permute-start(f32[128,512]{1,0:T(8,128)S(1)} %collective-permute-done.2.refs_0_), channel_id=1, source_target_pairs={{4,0},{8,12},{5,1},{9,13},{6,2},{10,14},{7,3},{11,15},{20,16},{24,... | collective-permute-start | bytes 786440 | tf_op jit(solution)/shard_map/ppermute | solution.py:61
  30.3 8.4 %collective-permute-done.10.refs_7_ = f32[128,512]{1,0:T(8,128)S(1)} collective-permute-done((f32[128,512]{1,0:T(8,128)S(1)}, f32[128,512]{1,0:T(8,128)S(1)}, u32[]{:S(2)}, u32[]{:S(2)}) %collective-permute-start.10) | collective-permute-done | bytes 262176 | tf_op jit(solution)/shard_map/ppermute | solution.py:61
  38.7 5.6 %collective-permute-done.6.refs_3_ = f32[128,512]{1,0:T(8,128)S(1)} collective-permute-done((f32[128,512]{1,0:T(8,128)S(1)}, f32[128,512]{1,0:T(8,128)S(1)}, u32[]{:S(2)}, u32[]{:S(2)}) %collective-permute-start.6) | collective-permute-done | bytes 262176 | tf_op jit(solution)/shard_map/ppermute | solution.py:61
  44.3 1.7 %shard_map.147 = (f32[384,512]{1,0:T(8,128)S(1)}, f32[384,384]{1,0:T(8,128)S(1)}, f32[128,512]{1,0:T(8,128)S(1)}, f32[128,512]{1,0:T(8,128)S(1)}) custom-call(f32[128,512]{1,0:T(8,128)S(1)} %multiply_subtract_fusion.refs_0_, f32[128,512]{1,0:T(8,128)S(1)} %collective-permute-done.4.refs_1_, f32[128,512]{1,0:T(8,128)S(1)} %collective-permute-done.5.refs_2_, ...), custom_call_target="tpu_custom_call" | custom-call | flops 1207959552 | bytes 6359552 | tf_op jit(solution)/shard_map/pallas_call | solution.py:110
  46.1 3.9 %collective-permute-done.8.refs_5_ = f32[128,512]{1,0:T(8,128)S(1)} collective-permute-done((f32[128,512]{1,0:T(8,128)S(1)}, f32[128,512]{1,0:T(8,128)S(1)}, u32[]{:S(2)}, u32[]{:S(2)}) %collective-permute-start.8) | collective-permute-done | bytes 262176 | tf_op jit(solution)/shard_map/ppermute | solution.py:61
  49.9 4.0 %shard_map.148 = (f32[512,512]{1,0:T(8,128)S(1)}, f32[1,512]{1,0:T(1,128)S(1)}, bf16[512,128]{1,0:T(8,128)(2,1)S(1)}, bf16[512,128]{1,0:T(8,128)(2,1)S(1)}, f32[...) custom-call(f32[128,512]{1,0:T(8,128)S(1)} %multiply_subtract_fusion.refs_0_, ...), custom_call_target="tpu_custom_call" | custom-call | flops 2617245696 | bytes 5705728 | tf_op jit(solution)/shard_map/pallas_call | solution.py:110
  53.9 1.3 %collective-permute-done.3.refs_1_ = f32[128,512]{1,0:T(8,128)S(1)} collective-permute-done((f32[128,512]{1,0:T(8,128)S(1)}, f32[128,512]{1,0:T(8,128)S(1)}, u32[]{:S(2)}, u32[]{:S(2)}) %collective-permute-start.3) | collective-permute-done | bytes 262176 | tf_op jit(solution)/shard_map/ppermute | solution.py:61
  55.2 1.9 %shard_map.149 = (f32[1,128,512]{2,1,0:T(8,128)}, f32[1,128,512]{2,1,0:T(8,128)}, f32[1,128,512]{2,1,0:T(8,128)}, f32[1,512,512]{2,1,0:T(8,128)}, f32[1,512]{1,0:T(1,128)}) custom-call(f32[128,512]{1,0:T(8,128)S(1)} %collective-permute-done.2.refs_0_, f32[128,512]{1,0:T(8,128)S(1)} %collective-permute-done.3.refs_1_, ...), custom_call_target="tpu_custom_call" | custom-call | flops 402653184 | bytes 4591616 | tf_op jit(solution)/shard_map/pallas_call | solution.py:110
  (34 shorter events, 2.2 us)
Async XLA Ops:
  0.6 4.5 %copy-start.2 = (f32[1,128,512]{2,1,0:T(8,128)S(1)}, f32[1,128,512]{2,1,0:T(8,128)}, u32[]{:S(2)}) copy-start(f32[1,128,512]{2,1,0:T(8,128)} %p.1) | copy-start | bytes 786436
  0.6 4.5 %copy-start.3 = (f32[128,512]{1,0:T(8,128)S(1)}, f32[128,512]{1,0:T(8,128)}, u32[]{:S(2)}) copy-start(f32[128,512]{1,0:T(8,128)} %qb.1) | copy-start | bytes 786436
  0.7 4.5 %copy-start.4 = (f32[128,512]{1,0:T(8,128)S(1)}, f32[128,512]{1,0:T(8,128)}, u32[]{:S(2)}) copy-start(f32[128,512]{1,0:T(8,128)} %ub.1) | copy-start | bytes 786436
  0.7 1.0 %copy-start.6 = (f32[1,128,512]{2,1,0:T(8,128)S(1)}, f32[1,128,512]{2,1,0:T(8,128)}, u32[]{:S(2)}) copy-start(f32[1,128,512]{2,1,0:T(8,128)} %refs_12_.1) | copy-start | bytes 786436
  1.7 0.9 %copy-start.8 = (f32[1,128,512]{2,1,0:T(8,128)S(1)}, f32[1,128,512]{2,1,0:T(8,128)}, u32[]{:S(2)}) copy-start(f32[1,128,512]{2,1,0:T(8,128)} %refs_11_.1) | copy-start | bytes 786436
  2.7 7.3 %collective-permute-start = (f32[128,512]{1,0:T(8,128)S(1)}, f32[128,512]{1,0:T(8,128)S(1)}, u32[]{:S(2)}, u32[]{:S(2)}) collective-permute-start(f32[128,512]{1,0:T(8,128)S(1)} %shard_map.146), channel_id=1, source_target_pairs={{0,1},{1,2},{2,3},{4,5},{5,6},{6,7},{8,9},{9,10},{10,11},{12,13},{... | collective-permute-start | bytes 786440 | tf_op jit(solution)/shard_map/ppermute | solution.py:22
  5.1 1.2 %copy-start = (f32[1,512,512]{2,1,0:T(8,128)S(1)}, f32[1,512,512]{2,1,0:T(8,128)}, u32[]{:S(2)}) copy-start(f32[1,512,512]{2,1,0:T(8,128)} %refs_8_.3) | copy-start | bytes 3145732
  6.3 0.9 %copy-start.5 = (f32[1,128,512]{2,1,0:T(8,128)S(1)}, f32[1,128,512]{2,1,0:T(8,128)}, u32[]{:S(2)}) copy-start(f32[1,128,512]{2,1,0:T(8,128)} %refs_10_.1) | copy-start | bytes 786436
  8.6 35.7 %copy-start.1 = (f32[1,512,512]{2,1,0:T(8,128)S(1)}, f32[1,512,512]{2,1,0:T(8,128)}, u32[]{:S(2)}) copy-start(f32[1,512,512]{2,1,0:T(8,128)} %refs_8_.3) | copy-start | bytes 3145732
  9.9 34.4 %copy-start.7 = (f32[1,128,512]{2,1,0:T(8,128)S(1)}, f32[1,128,512]{2,1,0:T(8,128)}, u32[]{:S(2)}) copy-start(f32[1,128,512]{2,1,0:T(8,128)} %refs_12_.1) | copy-start | bytes 786436
  9.9 34.4 %copy-start.11 = (f32[1,512]{1,0:T(1,128)S(1)}, f32[1,512]{1,0:T(1,128)}, u32[]{:S(2)}) copy-start(f32[1,512]{1,0:T(1,128)} %refs_9_.3) | copy-start | bytes 6148
  9.9 34.4 %copy-start.13 = (f32[128,512]{1,0:T(8,128)S(1)}, f32[128,512]{1,0:T(8,128)}, u32[]{:S(2)}) copy-start(f32[128,512]{1,0:T(8,128)} %refs_14_.1) | copy-start | bytes 786436
  10.0 39.9 %copy-start.9 = (f32[128,512]{1,0:T(8,128)}, f32[128,512]{1,0:T(8,128)S(1)}, u32[]{:S(2)}) copy-start(f32[128,512]{1,0:T(8,128)S(1)} %multiply_subtract_fusion.refs_0_) | copy-start | bytes 786436
  10.0 8.7 %collective-permute-start.4 = (f32[128,512]{1,0:T(8,128)S(1)}, f32[128,512]{1,0:T(8,128)S(1)}, u32[]{:S(2)}, u32[]{:S(2)}) collective-permute-start(f32[128,512]{1,0:T(8,128)S(1)} %multiply_subtract_fusion.refs_0_), channel_id=1, source_target_pairs={{0,4},{4,0},{8,12},{12,8},{1,5},{5,1},{9,13},{13,9},{2,6},{6,2},{1... | collective-permute-start | bytes 786440 | tf_op jit(solution)/shard_map/ppermute | solution.py:61
  12.5 11.9 %collective-permute-start.1 = (f32[128,512]{1,0:T(8,128)S(1)}, f32[128,512]{1,0:T(8,128)S(1)}, u32[]{:S(2)}, u32[]{:S(2)}) collective-permute-start(f32[128,512]{1,0:T(8,128)S(1)} %bitcast.2), channel_id=1, source_target_pairs={{0,4},{4,0},{8,12},{12,8},{1,5},{5,1},{9,13},{13,9},{2,6},{6,2},{1... | collective-permute-start | bytes 786440 | tf_op jit(solution)/shard_map/ppermute | solution.py:61
  12.6 12.5 %collective-permute-start.9 = (f32[128,512]{1,0:T(8,128)S(1)}, f32[128,512]{1,0:T(8,128)S(1)}, u32[]{:S(2)}, u32[]{:S(2)}) collective-permute-start(f32[128,512]{1,0:T(8,128)S(1)} %bitcast.3), channel_id=1, source_target_pairs={{4,8},{8,4},{5,9},{9,5},{6,10},{10,6},{7,11},{11,7},{20,24},{24,20... | collective-permute-start | bytes 786440 | tf_op jit(solution)/shard_map/ppermute | solution.py:61
  13.2 13.1 %collective-permute-start.5 = (f32[128,512]{1,0:T(8,128)S(1)}, f32[128,512]{1,0:T(8,128)S(1)}, u32[]{:S(2)}, u32[]{:S(2)}) collective-permute-start(f32[128,512]{1,0:T(8,128)S(1)} %multiply_subtract_fusion.refs_0_), channel_id=1, source_target_pairs={{4,8},{8,4},{5,9},{9,5},{6,10},{10,6},{7,11},{11,7},{20,24},{24,20... | collective-permute-start | bytes 786440 | tf_op jit(solution)/shard_map/ppermute | solution.py:61
  18.7 8.9 %collective-permute-start.7 = (f32[128,512]{1,0:T(8,128)S(1)}, f32[128,512]{1,0:T(8,128)S(1)}, u32[]{:S(2)}, u32[]{:S(2)}) collective-permute-start(f32[128,512]{1,0:T(8,128)S(1)} %collective-permute-done.4.refs_1_), channel_id=1, source_target_pairs={{4,8},{8,4},{5,9},{9,5},{6,10},{10,6},{7,11},{11,7},{20,24},{24,20... | collective-permute-start | bytes 786440 | tf_op jit(solution)/shard_map/ppermute | solution.py:61
  19.4 10.9 %collective-permute-start.11 = (f32[128,512]{1,0:T(8,128)S(1)}, f32[128,512]{1,0:T(8,128)S(1)}, u32[]{:S(2)}, u32[]{:S(2)}) collective-permute-start(f32[128,512]{1,0:T(8,128)S(1)} %multiply_subtract_fusion.refs_0_), channel_id=1, source_target_pairs={{1,0},{2,1},{3,2},{5,4},{6,5},{7,6},{9,8},{10,9},{11,10},{13,12},{... | collective-permute-start | bytes 786440 | tf_op jit(solution)/shard_map/ppermute | solution.py:22
  24.3 4.6 %collective-permute-start.2 = (f32[128,512]{1,0:T(8,128)S(1)}, f32[128,512]{1,0:T(8,128)S(1)}, u32[]{:S(2)}, u32[]{:S(2)}) collective-permute-start(f32[128,512]{1,0:T(8,128)S(1)} %collective-permute-done.1.refs_5_), channel_id=1, source_target_pairs={{4,8},{8,4},{5,9},{9,5},{6,10},{10,6},{7,11},{11,7},{20,24},{24,20... | collective-permute-start | bytes 786440 | tf_op jit(solution)/shard_map/ppermute | solution.py:61
  25.0 13.7 %collective-permute-start.10 = (f32[128,512]{1,0:T(8,128)S(1)}, f32[128,512]{1,0:T(8,128)S(1)}, u32[]{:S(2)}, u32[]{:S(2)}) collective-permute-start(f32[128,512]{1,0:T(8,128)S(1)} %collective-permute-done.9.refs_6_), channel_id=1, source_target_pairs={{4,0},{8,12},{5,1},{9,13},{6,2},{10,14},{7,3},{11,15},{20,16},{24,... | collective-permute-start | bytes 786440 | tf_op jit(solution)/shard_map/ppermute | solution.py:61
  26.3 18.0 %collective-permute-start.6 = (f32[128,512]{1,0:T(8,128)S(1)}, f32[128,512]{1,0:T(8,128)S(1)}, u32[]{:S(2)}, u32[]{:S(2)}) collective-permute-start(f32[128,512]{1,0:T(8,128)S(1)} %collective-permute-done.5.refs_2_), channel_id=1, source_target_pairs={{4,0},{8,12},{5,1},{9,13},{6,2},{10,14},{7,3},{11,15},{20,16},{24,... | collective-permute-start | bytes 786440 | tf_op jit(solution)/shard_map/ppermute | solution.py:61
  27.6 22.3 %collective-permute-start.8 = (f32[128,512]{1,0:T(8,128)S(1)}, f32[128,512]{1,0:T(8,128)S(1)}, u32[]{:S(2)}, u32[]{:S(2)}) collective-permute-start(f32[128,512]{1,0:T(8,128)S(1)} %collective-permute-done.7.refs_4_), channel_id=1, source_target_pairs={{4,0},{8,12},{5,1},{9,13},{6,2},{10,14},{7,3},{11,15},{20,16},{24,... | collective-permute-start | bytes 786440 | tf_op jit(solution)/shard_map/ppermute | solution.py:61
  29.0 26.2 %collective-permute-start.3 = (f32[128,512]{1,0:T(8,128)S(1)}, f32[128,512]{1,0:T(8,128)S(1)}, u32[]{:S(2)}, u32[]{:S(2)}) collective-permute-start(f32[128,512]{1,0:T(8,128)S(1)} %collective-permute-done.2.refs_0_), channel_id=1, source_target_pairs={{4,0},{8,12},{5,1},{9,13},{6,2},{10,14},{7,3},{11,15},{20,16},{24,... | collective-permute-start | bytes 786440 | tf_op jit(solution)/shard_map/ppermute | solution.py:61
  (2 other events, 1.3 us)
where the time goes:
time: 57.5 us; the launch traced here: 57.1 us
  waiting for transfers between devices  27.7 us (48%)
  starting transfers between devices  14.1 us (25%)
  Pallas kernels  8.84 us (15%)
  local copies, waits for them, and re-layouts  5.51 us (10%)
  between operations  0.91 us (2%)
    ppermute x10, waiting for transfers between devices, gather_line(): arrived = lax.ppermute(payload, axis, [(s, t) for s, t, _ in sends])  27.7 us
    ppermute x10, starting transfers between devices, gather_line(): arrived = lax.ppermute(payload, axis, [(s, t) for s, t, _ in sends])  10.4 us
    pallas_call x5, Pallas kernels, run(): pl.pallas_call(kernel, out_shape=outs, in_specs=[VMEM] * len(args), out_s...  8.84 us
    unnamed x28, local copies, waits for them, and re-layouts  5.51 us
    ppermute x2, starting transfers between devices, from_behind(): return lax.ppermute(x, axis, pairs)  3.7 us
  transfers between devices with their start and end apart: 12, of which 6 were waited for; matrix products, arithmetic and copies ran while one was open for 0% of the time, Pallas kernels for 12%

commit v1 on v0

--- a/solution.py
+++ b/solution.py
@@ -43,6 +43,22 @@
     return rounds
 
 
+def whole_swap(swaps):
+    layers = lax.axis_size("layer")
+    pairs = []
+    for i in range(lax.axis_size("dp")):
+        for l in range(layers):
+            partner = l ^ 1 if layers % 2 == 0 else l
+            there = (swaps[i], l) if i in swaps else (i, partner)
+            pairs.append((i * layers + l, there[0] * layers + there[1]))
+    return pairs
+
+
+def around(x, by):
+    count = lax.axis_size("layer")
+    return lax.ppermute(x, "layer", [(i, (i + by) % count) for i in range(count)])
+
+
 def gather_line(own, axis):
     count = lax.axis_size(axis)
     me = lax.axis_index(axis)
@@ -58,15 +74,15 @@
         for value, sources in others:
             mine = jnp.any(jnp.asarray(sources) == me)
             payload = jnp.where(mine, value, payload)
-        arrived = lax.ppermute(payload, axis, [(s, t) for s, t, _ in sends])
-        filled = []
+        swaps = dict((s, t) for s, t, _ in sends) | dict((t, s) for s, t, _ in sends)
+        arrived = lax.ppermute(payload, ("dp", "layer"), whole_swap(swaps))
+        filled = {}
         for source, target, block in sends:
             held[target, block] = arrived
-            if got[target] not in filled:
-                filled.append(got[target])
+            filled.setdefault(got[target], []).append(target)
             got[target] += 1
-        for slot in filled:
-            slots[slot].append(arrived)
+        for slot, members in filled.items():
+            slots[slot].append((arrived, members))
     return slots
 
 
@@ -105,16 +121,16 @@
     return jax.ShapeDtypeStruct(shape, jnp.bfloat16)
 
 
-def run(kernel, args, outs, flops, out_specs=None, scratch=()):
+def run(kernel, args, outs, flops, in_specs=None, out_specs=None, scratch=(), limit=24 * 2**20):
     nbytes = sum(x.size * x.dtype.itemsize for x in (*args, *outs))
     return pl.pallas_call(
         kernel,
         out_shape=outs,
-        in_specs=[VMEM] * len(args),
+        in_specs=[VMEM] * len(args) if in_specs is None else in_specs,
         out_specs=[VMEM] * len(outs) if out_specs is None else out_specs,
         scratch_shapes=scratch,
         cost_estimate=pl.CostEstimate(flops=flops, bytes_accessed=nbytes, transcendentals=0),
-        compiler_params=pltpu.CompilerParams(vmem_limit_bytes=24 * 2**20),
+        compiler_params=pltpu.CompilerParams(vmem_limit_bytes=limit),
     )(*args)
 
 
@@ -142,25 +158,57 @@
     return jnp.maximum(v, 0.0) + jnp.log1p(jnp.exp(-jnp.abs(v)))
 
 
-def minus_kernel(u, q, out):
+def fetch(sources, targets, sems):
+    copies = [pltpu.make_async_copy(s, t, sems.at[i]) for i, (s, t) in enumerate(zip(sources, targets))]
+    for copy in copies:
+        copy.start()
+    return copies
+
+
+def fetched(kernel, args, outs, flops):
+    room = [pltpu.VMEM(x.shape, x.dtype) for x in args]
+    args = [pltpu.with_memory_space_constraint(x, pltpu.HBM) for x in args]
+    return run(
+        kernel, args, outs, flops, in_specs=[HBM] * len(args),
+        scratch=room + [pltpu.SemaphoreType.DMA((len(args),))],
+    )
+
+
+def minus_kernel(u_in, q_in, out, u, q, sems):
+    for copy in fetch((u_in, q_in), (u, q), sems):
+        copy.wait()
     out[...] = u[0] - penalty_rho * q[0]
 
 
-def input_kernel(p, z, w, b, qb, ub, order, out):
+def input_kernel(*refs):
+    ins, out, room, sems = refs[:7], refs[7], refs[8:15], refs[15]
+    p, w, b, z, order, qb, ub = room
+    copies = fetch(ins, room, sems)
+    copies[0].wait()
+    left = split(p[0])
+    copies[1].wait()
     weight = split(w[0])
-    residual = dot3(split(p[0]), weight) + b[...] - z[0]
+    for copy in copies[2:4]:
+        copy.wait()
+    residual = dot3(left, weight) + b[...] - z[0]
     step = penalty_nu * dot3(split(residual), weight, NT) + penalty_rho * p[0]
     out[...] = p[0] - step_input * step
+    for copy in copies[4:]:
+        copy.wait()
 
     @pl.when(lax.axis_index("layer") == 0)
     def _():
         out[...] -= step_input * pick_rows(ub[...] - penalty_rho * qb[...], order[...])
 
 
-def total_of(refs):
+def block_of(refs, members):
     value = refs[0][...]
-    for ref in refs[1:]:
-        value = value + ref[...]
+    me = lax.axis_index("dp")
+    for ref, those in zip(refs[1:], members[1:]):
+        here = me == those[0]
+        for other in those[1:]:
+            here = jnp.logical_or(here, me == other)
+        value = jnp.where(here, ref[...], value)
     return value
 
 
@@ -168,6 +216,9 @@
     rows, width = inputs.shape
     early_count = rows * len(p_slots)
     count = early_count + rows
+    members = [[None]] + [[those for _, those in parts] for parts in p_slots]
+    p_slots = [[x for x, _ in parts] for parts in p_slots]
+    z_slots = [[x for x, _ in parts] for parts in z_slots]
     p_early = [[inputs]] + p_slots[:-1]
     z_early = [[preact[0]]] + z_slots[:-1]
     p_late, z_late = p_slots[-1], z_slots[-1]
@@ -187,10 +238,10 @@
         residual, kernel, z_part, q_part = refs[2 * sum(sizes) + 8 :]
         p_refs, z_refs = group(ins[: sum(sizes)], sizes), group(ins[sum(sizes) :], sizes)
         wide = split(w[0])
-        blocks = [split(total_of(r)) for r in p_refs]
+        blocks = [split(block_of(r, m)) for r, m in zip(p_refs, members)]
         for i, block in enumerate(blocks):
             at = slice(i * rows, (i + 1) * rows)
-            residual[at] = dot3(block, wide) + b[...] - total_of(z_refs[i])
+            residual[at] = dot3(block, wide) + b[...] - block_of(z_refs[i], members[i])
             for j in range(i + 1):
                 to = slice(j * rows, (j + 1) * rows)
                 piece = scale * (dot3(block, blocks[j], NT) + 1.0)
@@ -201,11 +252,9 @@
         z_part[...] = (1 - step_preact) * value - step_preact * (
             (softplus(value) - q[0]) * jax.nn.sigmoid(value)
         )
-        q_part[...] = u[0] + penalty_rho * pn[...]
-
-        @pl.when(lax.axis_index("layer") == lax.axis_size("layer") - 1)
-        def _():
-            q_part[...] += penalty_rho * pick_rows(pb[...], order[...])
+        last = lax.axis_index("layer") == lax.axis_size("layer") - 1
+        after = jnp.where(last, pick_rows(pb[...], order[...]), pn[...])
+        q_part[...] = u[0] + penalty_rho * after
 
     args = [x for parts in p_early for x in parts] + [x for parts in z_early for x in parts]
     args += [weight, offset, preact, outputs, duals, after_in, next_inputs, row_order]
@@ -222,7 +271,7 @@
         w_part, b_part, pull_high, pull_low, weigh, a_part, a_pull = refs[len(ins) + 4 : len(ins) + 11]
         j_ref, turned = refs[len(ins) + 11 :]
         wide = split(w[0])
-        every = [total_of(r) for r in group(ins, sizes + [len(p_late)])]
+        every = [block_of(r, m) for r, m in zip(group(ins, sizes + [len(p_late)]), members)]
         late = split(every[-1])
         j_ref[:early_count, :early_count] = kernel[...]
         for i, block in enumerate(every):
@@ -278,7 +327,7 @@
         ]
         z_out, q_out, u_out, w_out, b_out = refs[len(z_late) + 9 : len(z_late) + 14]
         z_own, q_own, u_own, w_own, b_own, sems = refs[len(z_late) + 14 :]
-        value = total_of(late_refs)
+        value = block_of(late_refs, members[-1])
         late = split(value)
         new_w = w_part[...] + dot3((pull_high[...], pull_low[...]), late)
         w_own[0] = new_w
@@ -324,17 +373,17 @@
     scale = step_weight / (rows * lax.axis_size("dp"))
     unit = 2 * rows * width * width * 3
     z_slots = gather_line(pre_acts[0], "dp")
-    (before,) = run(minus_kernel, (multipliers, layer_outputs), [f32(rows, width)], unit // 10)
-    before = from_behind(before, "layer", 1)
-    (inputs,) = run(
+    (before,) = fetched(minus_kernel, (multipliers, layer_outputs), [f32(rows, width)], unit // 10)
+    before = around(before, 1)
+    (inputs,) = fetched(
         input_kernel,
-        (layer_inputs, pre_acts, weights, biases, prev_outputs, prev_multipliers, row_order),
+        (layer_inputs, weights, biases, pre_acts, row_order, prev_outputs, prev_multipliers),
         [f32(rows, width)],
         unit * 2,
     )
-    inputs = inputs - step_input * before
+    inputs = inputs - step_input * jnp.where(lax.axis_index("layer") == 0, 0.0, before)
     p_slots = gather_line(inputs, "dp")
-    after_in = from_behind(inputs, "layer", -1)
+    after_in = around(inputs, -1)
     z, q, u, w, b = gathered_pass(
         inputs, pre_acts, layer_outputs, multipliers, weights, biases,
         after_in, next_inputs, row_order, p_slots, z_slots, scale,

time: 57.5 us -> 49.7 us (0.86)
  waiting for transfers between devices: 27.7 us -> 17.3 us
  starting transfers between devices: 14.1 us -> 19.8 us
  local copies, waits for them, and re-layouts: 5.51 us -> 0.04 us
  Pallas kernels: 8.84 us -> 11.7 us
    ppermute x12, waiting for transfers between devices: 27.7 us -> 17.3 us  [the longest x10 14.3 us: gather_line(): arrived = lax.ppermute(payload, ('dp', 'layer'), whole_swap(swaps))]
    ppermute x12, starting transfers between devices: 14.1 us -> 19.8 us  [the longest x10 17.3 us: gather_line(): arrived = lax.ppermute(payload, ('dp', 'layer'), whole_swap(swaps))]
    unnamed x28 -> x16, local copies, waits for them, and re-layouts: 5.51 us -> 0.04 us
    pallas_call x5, Pallas kernels: 8.84 us -> 11.7 us  [run(): pl.pallas_call(kernel, out_shape=outs, in_specs=[VMEM] * len(args) if in_...]
  transfers between devices with their start and end apart: 12 -> 12, of which waited for: 6 -> 5; matrix products, arithmetic and copies ran while one was open for 0% -> 0% of each run, Pallas kernels for 12% -> 18%
where the time goes in v1:
time: 49.7 us; the launch traced here: 49.6 us
  starting transfers between devices  19.8 us (40%)
  waiting for transfers between devices  17.3 us (35%)
  Pallas kernels  11.7 us (24%)
  between operations  0.75 us (2%)
    ppermute x10, starting transfers between devices, gather_line(): arrived = lax.ppermute(payload, ('dp', 'layer'), whole_swap(swaps))  17.3 us
    ppermute x10, waiting for transfers between devices, gather_line(): arrived = lax.ppermute(payload, ('dp', 'layer'), whole_swap(swaps))  14.3 us
    pallas_call x5, Pallas kernels, run(): pl.pallas_call(kernel, out_shape=outs, in_specs=[VMEM] * len(args) if in_...  11.7 us
    ppermute x2, waiting for transfers between devices, around(): lax.ppermute(x, 'layer', [(i, (i + by) % count) for i in range(count)])  3.01 us
    ppermute x2, starting transfers between devices, around(): lax.ppermute(x, 'layer', [(i, (i + by) % count) for i in range(count)])  2.44 us
  transfers between devices with their start and end apart: 12, of which 5 were waited for; matrix products, arithmetic and copies ran while one was open for 0% of the time, Pallas kernels for 18%

profile of v1, /device:TPU:0, one launch (start us, length us, event | category | flops | bytes accessed | tf_op | source)
XLA Modules:
  0.0 49.6 jit_solution(7748506154579995291)
XLA Ops:
  0.6 1.1 %shard_map.146 = f32[128,512]{1,0:T(8,128)S(1)} custom-call(f32[1,128,512]{2,1,0:T(8,128)} %refs_12_.1, f32[1,128,512]{2,1,0:T(8,128)} %refs_11_.1), custom_call_target="tpu_custom_call" | custom-call | flops 20132660 | bytes 786432 | tf_op jit(solution)/shard_map/pallas_call | solution.py:126
  1.7 0.5 %collective-permute-start = (f32[128,512]{1,0:T(8,128)S(1)}, f32[128,512]{1,0:T(8,128)S(1)}, u32[]{:S(2)}, u32[]{:S(2)}) collective-permute-start(f32[128,512]{1,0:T(8,128)S(1)} %shard_map.146), channel_id=1, source_target_pairs={{0,1},{1,2},{2,3},{3,0},{4,5},{5,6},{6,7},{7,4},{8,9},{9,10},{10,1... | collective-permute-start | bytes 786440 | tf_op jit(solution)/shard_map/ppermute | solution.py:59
  2.3 2.9 %shard_map.145 = f32[128,512]{1,0:T(8,128)S(1)} custom-call(f32[1,128,512]{2,1,0:T(8,128)} %refs_0_.1, f32[1,512,512]{2,1,0:T(8,128)} %refs_8_.3, f32[1,512]{1,0:T(1,128)} %refs_9_.3, f32[1,128,512]{2,1,0:T(8,128)} %refs_10_.1, s32[1,128]{1,0:T(1,128)} %refs_15_.1, f32[128,512]{1,0:T(8,128)} %refs_5_.1, f32[128,512]{1,0:T(8,128)} %refs_6_.1), custom_call_target="tpu_custom_call" | custom-call | flops 402653184 | bytes 2361856 | tf_op jit(solution)/shard_map/pallas_call | solution.py:126
  5.2 0.0 copy-start.1
  5.2 0.0 copy-start.2
  5.2 0.0 copy-start.3
  5.2 3.0 %collective-permute-done = f32[128,512]{1,0:T(8,128)S(1)} collective-permute-done((f32[128,512]{1,0:T(8,128)S(1)}, f32[128,512]{1,0:T(8,128)S(1)}, u32[]{:S(2)}, u32[]{:S(2)}) %collective-permute-start) | collective-permute-done | bytes 262176 | tf_op jit(solution)/shard_map/ppermute | solution.py:59
  8.3 0.0 copy-start.4
  8.3 2.5 %collective-permute-start.4 = (f32[128,512]{1,0:T(8,128)S(1)}, f32[128,512]{1,0:T(8,128)S(1)}, u32[]{:S(2)}, u32[]{:S(2)}) collective-permute-start(f32[128,512]{1,0:T(8,128)S(1)} %multiply_subtract_fusion.refs_0_), channel_id=1, source_target_pairs={{0,4},{1,5},{2,6},{3,7},{4,0},{5,1},{6,2},{7,3},{8,12},{9,13},{10,... | collective-permute-start | bytes 786440 | tf_op jit(solution)/shard_map/ppermute | solution.py:78
  10.7 0.1 collective-permute-start.1
  10.8 0.5 %collective-permute-start.5 = (f32[128,512]{1,0:T(8,128)S(1)}, f32[128,512]{1,0:T(8,128)S(1)}, u32[]{:S(2)}, u32[]{:S(2)}) collective-permute-start(f32[128,512]{1,0:T(8,128)S(1)} %multiply_subtract_fusion.refs_0_), channel_id=1, source_target_pairs={{0,1},{1,0},{2,3},{3,2},{4,8},{5,9},{6,10},{7,11},{8,4},{9,5},{10,... | collective-permute-start | bytes 786440 | tf_op jit(solution)/shard_map/ppermute | solution.py:78
  11.3 6.6 %collective-permute-done.4.refs_1_ = f32[128,512]{1,0:T(8,128)S(1)} collective-permute-done((f32[128,512]{1,0:T(8,128)S(1)}, f32[128,512]{1,0:T(8,128)S(1)}, u32[]{:S(2)}, u32[]{:S(2)}) %collective-permute-start.4) | collective-permute-done | bytes 262176 | tf_op jit(solution)/shard_map/ppermute | solution.py:78
  17.9 1.9 %collective-permute-start.11 = (f32[128,512]{1,0:T(8,128)S(1)}, f32[128,512]{1,0:T(8,128)S(1)}, u32[]{:S(2)}, u32[]{:S(2)}) collective-permute-start(f32[128,512]{1,0:T(8,128)S(1)} %multiply_subtract_fusion.refs_0_), channel_id=1, source_target_pairs={{0,3},{1,0},{2,1},{3,2},{4,7},{5,4},{6,5},{7,6},{8,11},{9,8},{10,9... | collective-permute-start | bytes 786440 | tf_op jit(solution)/shard_map/ppermute | solution.py:59
  19.8 2.3 %collective-permute-done.1.refs_5_ = f32[128,512]{1,0:T(8,128)S(1)} collective-permute-done((f32[128,512]{1,0:T(8,128)S(1)}, f32[128,512]{1,0:T(8,128)S(1)}, u32[]{:S(2)}, u32[]{:S(2)}) %collective-permute-start.1) | collective-permute-done | bytes 262176 | tf_op jit(solution)/shard_map/ppermute | solution.py:78
  22.1 3.2 %collective-permute-start.10 = (f32[128,512]{1,0:T(8,128)S(1)}, f32[128,512]{1,0:T(8,128)S(1)}, u32[]{:S(2)}, u32[]{:S(2)}) collective-permute-start(f32[128,512]{1,0:T(8,128)S(1)} %collective-permute-done.9.refs_6_), channel_id=1, source_target_pairs={{0,4},{1,5},{2,6},{3,7},{4,0},{5,1},{6,2},{7,3},{8,12},{9,13},{10,... | collective-permute-start | bytes 786440 | tf_op jit(solution)/shard_map/ppermute | solution.py:78
  25.3 2.3 %collective-permute-start.6 = (f32[128,512]{1,0:T(8,128)S(1)}, f32[128,512]{1,0:T(8,128)S(1)}, u32[]{:S(2)}, u32[]{:S(2)}) collective-permute-start(f32[128,512]{1,0:T(8,128)S(1)} %collective-permute-done.5.refs_2_), channel_id=1, source_target_pairs={{0,4},{1,5},{2,6},{3,7},{4,0},{5,1},{6,2},{7,3},{8,12},{9,13},{10,... | collective-permute-start | bytes 786440 | tf_op jit(solution)/shard_map/ppermute | solution.py:78
  27.6 5.6 %collective-permute-start.8 = (f32[128,512]{1,0:T(8,128)S(1)}, f32[128,512]{1,0:T(8,128)S(1)}, u32[]{:S(2)}, u32[]{:S(2)}) collective-permute-start(f32[128,512]{1,0:T(8,128)S(1)} %collective-permute-done.7.refs_4_), channel_id=1, source_target_pairs={{0,4},{1,5},{2,6},{3,7},{4,0},{5,1},{6,2},{7,3},{8,12},{9,13},{10,... | collective-permute-start | bytes 786440 | tf_op jit(solution)/shard_map/ppermute | solution.py:78
  33.2 3.2 %collective-permute-start.3 = (f32[128,512]{1,0:T(8,128)S(1)}, f32[128,512]{1,0:T(8,128)S(1)}, u32[]{:S(2)}, u32[]{:S(2)}) collective-permute-start(f32[128,512]{1,0:T(8,128)S(1)} %collective-permute-done.2.refs_0_), channel_id=1, source_target_pairs={{0,4},{1,5},{2,6},{3,7},{4,0},{5,1},{6,2},{7,3},{8,12},{9,13},{10,... | collective-permute-start | bytes 786440 | tf_op jit(solution)/shard_map/ppermute | solution.py:78
  36.4 1.6 %collective-permute-done.6.refs_3_ = f32[128,512]{1,0:T(8,128)S(1)} collective-permute-done((f32[128,512]{1,0:T(8,128)S(1)}, f32[128,512]{1,0:T(8,128)S(1)}, u32[]{:S(2)}, u32[]{:S(2)}) %collective-permute-start.6) | collective-permute-done | bytes 262176 | tf_op jit(solution)/shard_map/ppermute | solution.py:78
  38.1 1.8 %shard_map.147 = (f32[384,512]{1,0:T(8,128)S(1)}, f32[384,384]{1,0:T(8,128)S(1)}, f32[128,512]{1,0:T(8,128)S(1)}, f32[128,512]{1,0:T(8,128)S(1)}) custom-call(f32[128,512]{1,0:T(8,128)S(1)} %multiply_subtract_fusion.refs_0_, f32[128,512]{1,0:T(8,128)S(1)} %collective-permute-done.4.refs_1_, f32[128,512]{1,0:T(8,128)S(1)} %collective-permute-done.5.refs_2_, ...), custom_call_target="tpu_custom_call" | custom-call | flops 1207959552 | bytes 6359552 | tf_op jit(solution)/shard_map/pallas_call | solution.py:126
  40.0 3.7 %collective-permute-done.8.refs_5_ = f32[128,512]{1,0:T(8,128)S(1)} collective-permute-done((f32[128,512]{1,0:T(8,128)S(1)}, f32[128,512]{1,0:T(8,128)S(1)}, u32[]{:S(2)}, u32[]{:S(2)}) %collective-permute-start.8) | collective-permute-done | bytes 262176 | tf_op jit(solution)/shard_map/ppermute | solution.py:78
  43.7 4.0 %shard_map.148 = (f32[512,512]{1,0:T(8,128)S(1)}, f32[1,512]{1,0:T(1,128)S(1)}, bf16[512,128]{1,0:T(8,128)(2,1)S(1)}, bf16[512,128]{1,0:T(8,128)(2,1)S(1)}, f32[...) custom-call(f32[128,512]{1,0:T(8,128)S(1)} %multiply_subtract_fusion.refs_0_, ...), custom_call_target="tpu_custom_call" | custom-call | flops 2617245696 | bytes 5705728 | tf_op jit(solution)/shard_map/pallas_call | solution.py:126
  47.7 0.0 collective-permute-done.3.refs_1_
  47.7 1.9 %shard_map.149 = (f32[1,128,512]{2,1,0:T(8,128)}, f32[1,128,512]{2,1,0:T(8,128)}, f32[1,128,512]{2,1,0:T(8,128)}, f32[1,512,512]{2,1,0:T(8,128)}, f32[1,512]{1,0:T(1,128)}) custom-call(f32[128,512]{1,0:T(8,128)S(1)} %collective-permute-done.2.refs_0_, f32[128,512]{1,0:T(8,128)S(1)} %collective-permute-done.3.refs_1_, ...), custom_call_target="tpu_custom_call" | custom-call | flops 402653184 | bytes 4591616 | tf_op jit(solution)/shard_map/pallas_call | solution.py:126
  (22 shorter events, 0.1 us)
Async XLA Ops:
  1.7 6.5 %collective-permute-start = (f32[128,512]{1,0:T(8,128)S(1)}, f32[128,512]{1,0:T(8,128)S(1)}, u32[]{:S(2)}, u32[]{:S(2)}) collective-permute-start(f32[128,512]{1,0:T(8,128)S(1)} %shard_map.146), channel_id=1, source_target_pairs={{0,1},{1,2},{2,3},{3,0},{4,5},{5,6},{6,7},{7,4},{8,9},{9,10},{10,1... | collective-permute-start | bytes 786440 | tf_op jit(solution)/shard_map/ppermute | solution.py:59
  2.3 35.8 %copy-start = (f32[1,512,512]{2,1,0:T(8,128)S(1)}, f32[1,512,512]{2,1,0:T(8,128)}, u32[]{:S(2)}) copy-start(f32[1,512,512]{2,1,0:T(8,128)} %refs_8_.3) | copy-start | bytes 3145732
  2.3 35.8 %copy-start.6 = (s32[1,128]{1,0:T(1,128)S(1)}, s32[1,128]{1,0:T(1,128)}, u32[]{:S(2)}) copy-start(s32[1,128]{1,0:T(1,128)} %refs_15_.1) | copy-start | bytes 1540
  2.3 35.8 %copy-start.7 = (f32[128,512]{1,0:T(8,128)S(1)}, f32[128,512]{1,0:T(8,128)}, u32[]{:S(2)}) copy-start(f32[128,512]{1,0:T(8,128)} %refs_14_.1) | copy-start | bytes 786436
  5.2 5.6 %copy-start.1 = (f32[1,128,512]{2,1,0:T(8,128)S(1)}, f32[1,128,512]{2,1,0:T(8,128)}, u32[]{:S(2)}) copy-start(f32[1,128,512]{2,1,0:T(8,128)} %refs_10_.1) | copy-start | bytes 786436
  5.2 32.9 %copy-start.2 = (f32[1,128,512]{2,1,0:T(8,128)S(1)}, f32[1,128,512]{2,1,0:T(8,128)}, u32[]{:S(2)}) copy-start(f32[1,128,512]{2,1,0:T(8,128)} %refs_12_.1) | copy-start | bytes 786436
  5.2 32.9 %copy-start.3 = (f32[1,128,512]{2,1,0:T(8,128)S(1)}, f32[1,128,512]{2,1,0:T(8,128)}, u32[]{:S(2)}) copy-start(f32[1,128,512]{2,1,0:T(8,128)} %refs_11_.1) | copy-start | bytes 786436
  5.2 32.9 %copy-start.5 = (f32[1,512]{1,0:T(1,128)S(1)}, f32[1,512]{1,0:T(1,128)}, u32[]{:S(2)}) copy-start(f32[1,512]{1,0:T(1,128)} %refs_9_.3) | copy-start | bytes 6148
  8.3 35.4 %copy-start.4 = (f32[128,512]{1,0:T(8,128)}, f32[128,512]{1,0:T(8,128)S(1)}, u32[]{:S(2)}) copy-start(f32[128,512]{1,0:T(8,128)S(1)} %multiply_subtract_fusion.refs_0_) | copy-start | bytes 786436
  8.3 9.6 %collective-permute-start.4 = (f32[128,512]{1,0:T(8,128)S(1)}, f32[128,512]{1,0:T(8,128)S(1)}, u32[]{:S(2)}, u32[]{:S(2)}) collective-permute-start(f32[128,512]{1,0:T(8,128)S(1)} %multiply_subtract_fusion.refs_0_), channel_id=1, source_target_pairs={{0,4},{1,5},{2,6},{3,7},{4,0},{5,1},{6,2},{7,3},{8,12},{9,13},{10,... | collective-permute-start | bytes 786440 | tf_op jit(solution)/shard_map/ppermute | solution.py:78
  10.7 11.4 %collective-permute-start.1 = (f32[128,512]{1,0:T(8,128)S(1)}, f32[128,512]{1,0:T(8,128)S(1)}, u32[]{:S(2)}, u32[]{:S(2)}) collective-permute-start(f32[128,512]{1,0:T(8,128)S(1)} %bitcast.2), channel_id=1, source_target_pairs={{0,4},{1,5},{2,6},{3,7},{4,0},{5,1},{6,2},{7,3},{8,12},{9,13},{10,... | collective-permute-start | bytes 786440 | tf_op jit(solution)/shard_map/ppermute | solution.py:78
  10.8 11.3 %collective-permute-start.9 = (f32[128,512]{1,0:T(8,128)S(1)}, f32[128,512]{1,0:T(8,128)S(1)}, u32[]{:S(2)}, u32[]{:S(2)}) collective-permute-start(f32[128,512]{1,0:T(8,128)S(1)} %bitcast.3), channel_id=1, source_target_pairs={{0,1},{1,0},{2,3},{3,2},{4,8},{5,9},{6,10},{7,11},{8,4},{9,5},{10,... | collective-permute-start | bytes 786440 | tf_op jit(solution)/shard_map/ppermute | solution.py:78
  10.8 14.4 %collective-permute-start.5 = (f32[128,512]{1,0:T(8,128)S(1)}, f32[128,512]{1,0:T(8,128)S(1)}, u32[]{:S(2)}, u32[]{:S(2)}) collective-permute-start(f32[128,512]{1,0:T(8,128)S(1)} %multiply_subtract_fusion.refs_0_), channel_id=1, source_target_pairs={{0,1},{1,0},{2,3},{3,2},{4,8},{5,9},{6,10},{7,11},{8,4},{9,5},{10,... | collective-permute-start | bytes 786440 | tf_op jit(solution)/shard_map/ppermute | solution.py:78
  17.9 9.7 %collective-permute-start.7 = (f32[128,512]{1,0:T(8,128)S(1)}, f32[128,512]{1,0:T(8,128)S(1)}, u32[]{:S(2)}, u32[]{:S(2)}) collective-permute-start(f32[128,512]{1,0:T(8,128)S(1)} %collective-permute-done.4.refs_1_), channel_id=1, source_target_pairs={{0,1},{1,0},{2,3},{3,2},{4,8},{5,9},{6,10},{7,11},{8,4},{9,5},{10,... | collective-permute-start | bytes 786440 | tf_op jit(solution)/shard_map/ppermute | solution.py:78
  17.9 18.5 %collective-permute-start.11 = (f32[128,512]{1,0:T(8,128)S(1)}, f32[128,512]{1,0:T(8,128)S(1)}, u32[]{:S(2)}, u32[]{:S(2)}) collective-permute-start(f32[128,512]{1,0:T(8,128)S(1)} %multiply_subtract_fusion.refs_0_), channel_id=1, source_target_pairs={{0,3},{1,0},{2,1},{3,2},{4,7},{5,4},{6,5},{7,6},{8,11},{9,8},{10,9... | collective-permute-start | bytes 786440 | tf_op jit(solution)/shard_map/ppermute | solution.py:59
  22.1 11.1 %collective-permute-start.2 = (f32[128,512]{1,0:T(8,128)S(1)}, f32[128,512]{1,0:T(8,128)S(1)}, u32[]{:S(2)}, u32[]{:S(2)}) collective-permute-start(f32[128,512]{1,0:T(8,128)S(1)} %collective-permute-done.1.refs_5_), channel_id=1, source_target_pairs={{0,1},{1,0},{2,3},{3,2},{4,8},{5,9},{6,10},{7,11},{8,4},{9,5},{10,... | collective-permute-start | bytes 786440 | tf_op jit(solution)/shard_map/ppermute | solution.py:78
  22.1 14.3 %collective-permute-start.10 = (f32[128,512]{1,0:T(8,128)S(1)}, f32[128,512]{1,0:T(8,128)S(1)}, u32[]{:S(2)}, u32[]{:S(2)}) collective-permute-start(f32[128,512]{1,0:T(8,128)S(1)} %collective-permute-done.9.refs_6_), channel_id=1, source_target_pairs={{0,4},{1,5},{2,6},{3,7},{4,0},{5,1},{6,2},{7,3},{8,12},{9,13},{10,... | collective-permute-start | bytes 786440 | tf_op jit(solution)/shard_map/ppermute | solution.py:78
  25.3 12.8 %collective-permute-start.6 = (f32[128,512]{1,0:T(8,128)S(1)}, f32[128,512]{1,0:T(8,128)S(1)}, u32[]{:S(2)}, u32[]{:S(2)}) collective-permute-start(f32[128,512]{1,0:T(8,128)S(1)} %collective-permute-done.5.refs_2_), channel_id=1, source_target_pairs={{0,4},{1,5},{2,6},{3,7},{4,0},{5,1},{6,2},{7,3},{8,12},{9,13},{10,... | collective-permute-start | bytes 786440 | tf_op jit(solution)/shard_map/ppermute | solution.py:78
  27.6 16.1 %collective-permute-start.8 = (f32[128,512]{1,0:T(8,128)S(1)}, f32[128,512]{1,0:T(8,128)S(1)}, u32[]{:S(2)}, u32[]{:S(2)}) collective-permute-start(f32[128,512]{1,0:T(8,128)S(1)} %collective-permute-done.7.refs_4_), channel_id=1, source_target_pairs={{0,4},{1,5},{2,6},{3,7},{4,0},{5,1},{6,2},{7,3},{8,12},{9,13},{10,... | collective-permute-start | bytes 786440 | tf_op jit(solution)/shard_map/ppermute | solution.py:78
  33.2 14.5 %collective-permute-start.3 = (f32[128,512]{1,0:T(8,128)S(1)}, f32[128,512]{1,0:T(8,128)S(1)}, u32[]{:S(2)}, u32[]{:S(2)}) collective-permute-start(f32[128,512]{1,0:T(8,128)S(1)} %collective-permute-done.2.refs_0_), channel_id=1, source_target_pairs={{0,4},{1,5},{2,6},{3,7},{4,0},{5,1},{6,2},{7,3},{8,12},{9,13},{10,... | collective-permute-start | bytes 786440 | tf_op jit(solution)/shard_map/ppermute | solution.py:78

commit v2 on v1

--- a/solution.py
+++ b/solution.py
@@ -155,7 +155,7 @@
 
 
 def softplus(v):
-    return jnp.maximum(v, 0.0) + jnp.log1p(jnp.exp(-jnp.abs(v)))
+    return jnp.maximum(v, 0.0) + jnp.log(1.0 + jnp.exp(-jnp.abs(v)))
 
 
 def fetch(sources, targets, sems):
@@ -165,36 +165,23 @@
     return copies
 
 
-def fetched(kernel, args, outs, flops):
-    room = [pltpu.VMEM(x.shape, x.dtype) for x in args]
-    args = [pltpu.with_memory_space_constraint(x, pltpu.HBM) for x in args]
-    return run(
-        kernel, args, outs, flops, in_specs=[HBM] * len(args),
-        scratch=room + [pltpu.SemaphoreType.DMA((len(args),))],
-    )
-
-
-def minus_kernel(u_in, q_in, out, u, q, sems):
-    for copy in fetch((u_in, q_in), (u, q), sems):
+def first_kernel(u_in, q_in, *refs):
+    count = (len(refs) - 4) // 2
+    sources, out, targets = refs[:count], refs[count], refs[count + 1 : 2 * count + 1]
+    u, q, sems = refs[2 * count + 1 :]
+    copies = fetch((u_in, q_in) + sources, (u, q) + targets, sems)
+    for copy in copies[:2]:
         copy.wait()
     out[...] = u[0] - penalty_rho * q[0]
-
-
-def input_kernel(*refs):
-    ins, out, room, sems = refs[:7], refs[7], refs[8:15], refs[15]
-    p, w, b, z, order, qb, ub = room
-    copies = fetch(ins, room, sems)
-    copies[0].wait()
-    left = split(p[0])
-    copies[1].wait()
+    for copy in copies[2:]:
+        copy.wait()
+
+
+def input_kernel(p, w, b, z, order, qb, ub, out):
     weight = split(w[0])
-    for copy in copies[2:4]:
-        copy.wait()
-    residual = dot3(left, weight) + b[...] - z[0]
+    residual = dot3(split(p[0]), weight) + b[...] - z[0]
     step = penalty_nu * dot3(split(residual), weight, NT) + penalty_rho * p[0]
     out[...] = p[0] - step_input * step
-    for copy in copies[4:]:
-        copy.wait()
 
     @pl.when(lax.axis_index("layer") == 0)
     def _():
@@ -320,6 +307,9 @@
         scratch=[pltpu.VMEM((count, count), jnp.float32), pltpu.VMEM((width, count), jnp.float32)],
     )
 
+    w_chunks = [slice(i * width // 4, (i + 1) * width // 4) for i in range(4)]
+    z_chunks = [slice(i * rows // 2, (i + 1) * rows // 2) for i in range(2)]
+
     def last_kernel(*refs):
         late_refs = refs[: len(z_late)]
         w_part, b_part, pull_high, pull_low, weigh, a_part, a_pull, z_part, q_part = refs[
@@ -329,27 +319,30 @@
         z_own, q_own, u_own, w_own, b_own, sems = refs[len(z_late) + 14 :]
         value = block_of(late_refs, members[-1])
         late = split(value)
-        new_w = w_part[...] + dot3((pull_high[...], pull_low[...]), late)
-        w_own[0] = new_w
-        copies = [pltpu.make_async_copy(w_own, w_out, sems.at[0])]
-        copies[-1].start()
+        copies = []
+
+        def send(own, out, at):
+            copies.append(pltpu.make_async_copy(own.at[0, at], out.at[0, at], sems.at[len(copies)]))
+            copies[-1].start()
+
+        for at in w_chunks:
+            w_own[0, at] = w_part[at] + dot3((pull_high[at], pull_low[at]), late)
+            send(w_own, w_out, at)
         shift = jnp.sum(weigh[:, :1] * value, axis=0, keepdims=True)
         b_own[...] = b_part[...] + shift
-        copies.append(pltpu.make_async_copy(b_own, b_out, sems.at[1]))
+        copies.append(pltpu.make_async_copy(b_own, b_out, sems.at[len(copies)]))
         copies[-1].start()
-        target = a_part[...] + shift + dot3(split(a_pull[...]), late)
-        new_z = z_part[...] + step_preact * target
-        z_own[0] = new_z
-        copies.append(pltpu.make_async_copy(z_own, z_out, sems.at[2]))
-        copies[-1].start()
-        both = q_part[...]
-        new_q = (penalty_nu * softplus(new_z) + both) / (penalty_nu + penalty_rho)
-        q_own[0] = new_q
-        copies.append(pltpu.make_async_copy(q_own, q_out, sems.at[3]))
-        copies[-1].start()
-        u_own[0] = both - penalty_rho * new_q
-        copies.append(pltpu.make_async_copy(u_own, u_out, sems.at[4]))
-        copies[-1].start()
+        for at in z_chunks:
+            target = a_part[at] + shift + dot3(split(a_pull[at]), late)
+            new_z = z_part[at] + step_preact * target
+            z_own[0, at] = new_z
+            send(z_own, z_out, at)
+            both = q_part[at]
+            new_q = (penalty_nu * softplus(new_z) + both) / (penalty_nu + penalty_rho)
+            q_own[0, at] = new_q
+            send(q_own, q_out, at)
+            u_own[0, at] = both - penalty_rho * new_q
+            send(u_own, u_out, at)
         for copy in copies:
             copy.wait()
 
@@ -361,7 +354,7 @@
         outs,
         unit * 2,
         out_specs=[HBM] * len(outs),
-        scratch=[pltpu.VMEM(o.shape, jnp.float32) for o in outs] + [pltpu.SemaphoreType.DMA((5,))],
+        scratch=[pltpu.VMEM(o.shape, jnp.float32) for o in outs] + [pltpu.SemaphoreType.DMA((len(w_chunks) + 3 * len(z_chunks) + 1,))],
     )
 
 
@@ -373,11 +366,24 @@
     scale = step_weight / (rows * lax.axis_size("dp"))
     unit = 2 * rows * width * width * 3
     z_slots = gather_line(pre_acts[0], "dp")
-    (before,) = fetched(minus_kernel, (multipliers, layer_outputs), [f32(rows, width)], unit // 10)
+    shared = (layer_inputs, weights, biases, pre_acts)
+    hbm = [
+        pltpu.with_memory_space_constraint(x, pltpu.HBM)
+        for x in (multipliers, layer_outputs) + shared
+    ]
+    one = pltpu.VMEM((1, rows, width), jnp.float32)
+    before, p_near, w_near, b_near, z_near = run(
+        first_kernel,
+        hbm,
+        [f32(rows, width)] + [f32(*x.shape) for x in shared],
+        unit // 10,
+        in_specs=[HBM] * len(hbm),
+        scratch=[one, one, pltpu.SemaphoreType.DMA((len(hbm),))],
+    )
     before = around(before, 1)
-    (inputs,) = fetched(
+    (inputs,) = run(
         input_kernel,
-        (layer_inputs, weights, biases, pre_acts, row_order, prev_outputs, prev_multipliers),
+        (p_near, w_near, b_near, z_near, row_order, prev_outputs, prev_multipliers),
         [f32(rows, width)],
         unit * 2,
     )
@@ -385,7 +391,7 @@
     p_slots = gather_line(inputs, "dp")
     after_in = around(inputs, -1)
     z, q, u, w, b = gathered_pass(
-        inputs, pre_acts, layer_outputs, multipliers, weights, biases,
+        inputs, z_near, layer_outputs, multipliers, w_near, b_near,
         after_in, next_inputs, row_order, p_slots, z_slots, scale,
     )
     return (inputs[None], z, q, u, w, b)

time: 49.7 us -> 50.1 us (level)
  Pallas kernels: 11.7 us -> 10.2 us
  waiting for transfers between devices: 17.3 us -> 18.5 us
  local copies, waits for them, and re-layouts: 0.04 us -> 0.69 us
    pallas_call x5, Pallas kernels: 11.7 us -> 10.2 us  [run(): pl.pallas_call(kernel, out_shape=outs, in_specs=[VMEM] * len(args) if in_...]
    ppermute x2, waiting for transfers between devices: 3.01 us -> 4.01 us  [around(): lax.ppermute(x, 'layer', [(i, (i + by) % count) for i in range(count)])]
    unnamed x16, local copies, waits for them, and re-layouts: 0.04 us -> 0.69 us
  transfers between devices with their start and end apart: 12 -> 12, of which waited for: 5 -> 6; matrix products, arithmetic and copies ran while one was open for 0% -> 0% of each run, Pallas kernels for 18% -> 14%
where the time goes in v2:
time: 50.1 us; the launch traced here: 49.9 us
  starting transfers between devices  19.8 us (40%)
  waiting for transfers between devices  18.5 us (37%)
  Pallas kernels  10.2 us (20%)
  between operations  0.73 us (1%)
  local copies, waits for them, and re-layouts  0.69 us (1%)
    ppermute x10, starting transfers between devices, gather_line(): arrived = lax.ppermute(payload, ('dp', 'layer'), whole_swap(swaps))  17.3 us
    ppermute x10, waiting for transfers between devices, gather_line(): arrived = lax.ppermute(payload, ('dp', 'layer'), whole_swap(swaps))  14.5 us
    pallas_call x5, Pallas kernels, run(): pl.pallas_call(kernel, out_shape=outs, in_specs=[VMEM] * len(args) if in_...  10.2 us
    ppermute x2, waiting for transfers between devices, around(): lax.ppermute(x, 'layer', [(i, (i + by) % count) for i in range(count)])  4.01 us
    ppermute x2, starting transfers between devices, around(): lax.ppermute(x, 'layer', [(i, (i + by) % count) for i in range(count)])  2.44 us
  transfers between devices with their start and end apart: 12, of which 6 were waited for; matrix products, arithmetic and copies ran while one was open for 0% of the time, Pallas kernels for 14%

profile of v2, /device:TPU:0, one launch (start us, length us, event | category | flops | bytes accessed | tf_op | source)
XLA Modules:
  0.0 49.9 jit_solution(7880548721992616997)
XLA Ops:
  0.7 1.6 %shard_map.145 = (f32[128,512]{1,0:T(8,128)S(1)}, f32[1,128,512]{2,1,0:T(8,128)S(1)}, f32[1,512,512]{2,1,0:T(8,128)S(1)}, f32[1,512]{1,0:T(1,128)S(1)}, f32[1,128,512]{2,1,0:T(8,128)S(1)}) custom-call(f32[1,128,512]{2,1,0:T(8,128)} %refs_12_.1, f32[1,128,512]{2,1,0:T(8,128)} %refs_11_.1, f32[1,128,512]{2,1,0:T(8,128)} %refs_0_.1, f32[1,512,512]{2,1,0:T(8,128)} %refs_1_.1, ...), custom_call_target="tpu_custom_call" | custom-call | flops 20132660 | bytes 3936256 | tf_op jit(solution)/shard_map/pallas_call | solution.py:126
  2.3 0.5 %collective-permute-start = (f32[128,512]{1,0:T(8,128)S(1)}, f32[128,512]{1,0:T(8,128)S(1)}, u32[]{:S(2)}, u32[]{:S(2)}) collective-permute-start(f32[128,512]{1,0:T(8,128)S(1)} %get-tuple-element.31), channel_id=1, source_target_pairs={{0,1},{1,2},{2,3},{3,0},{4,5},{5,6},{6,7},{7,4},{8,9},{9,10},{10,1... | collective-permute-start | bytes 786440 | tf_op jit(solution)/shard_map/ppermute | solution.py:59
  2.8 0.6 %copy-done.5 = s32[1,128]{1,0:T(1,128)S(1)} copy-done((s32[1,128]{1,0:T(1,128)S(1)}, s32[1,128]{1,0:T(1,128)}, u32[]{:S(2)}) %copy-start.5) | copy-done | bytes 536
  3.5 1.3 %shard_map.146 = f32[128,512]{1,0:T(8,128)S(1)} custom-call(f32[1,128,512]{2,1,0:T(8,128)S(1)} %get-tuple-element.27.p, f32[1,512,512]{2,1,0:T(8,128)S(1)} %get-tuple-element.28.w.refs_8_, f32[1,512]{1,0:T(1,128)S(1)} %get-tuple-element.29.b.refs_9_, f32[1,128,512]{2,1,0:T(8,128)S(1)} %get-tuple-element.30.z.refs_10_, s32[1,128]{1,0:T(1,128)S(1)} %copy-done.5, ...), custom_call_target="tpu_custom_call" | custom-call | flops 402653184 | bytes 2361856 | tf_op jit(solution)/shard_map/pallas_call | solution.py:126
  4.8 0.0 copy-start.3
  4.8 0.0 copy-start.6
  4.8 4.0 %collective-permute-done = f32[128,512]{1,0:T(8,128)S(1)} collective-permute-done((f32[128,512]{1,0:T(8,128)S(1)}, f32[128,512]{1,0:T(8,128)S(1)}, u32[]{:S(2)}, u32[]{:S(2)}) %collective-permute-start) | collective-permute-done | bytes 262176 | tf_op jit(solution)/shard_map/ppermute | solution.py:59
  8.9 0.0 copy-start.4
  8.9 2.5 %collective-permute-start.4 = (f32[128,512]{1,0:T(8,128)S(1)}, f32[128,512]{1,0:T(8,128)S(1)}, u32[]{:S(2)}, u32[]{:S(2)}) collective-permute-start(f32[128,512]{1,0:T(8,128)S(1)} %multiply_subtract_fusion.refs_0_), channel_id=1, source_target_pairs={{0,4},{1,5},{2,6},{3,7},{4,0},{5,1},{6,2},{7,3},{8,12},{9,13},{10,... | collective-permute-start | bytes 786440 | tf_op jit(solution)/shard_map/ppermute | solution.py:78
  11.3 0.1 collective-permute-start.1
  11.4 0.5 %collective-permute-start.5 = (f32[128,512]{1,0:T(8,128)S(1)}, f32[128,512]{1,0:T(8,128)S(1)}, u32[]{:S(2)}, u32[]{:S(2)}) collective-permute-start(f32[128,512]{1,0:T(8,128)S(1)} %multiply_subtract_fusion.refs_0_), channel_id=1, source_target_pairs={{0,1},{1,0},{2,3},{3,2},{4,8},{5,9},{6,10},{7,11},{8,4},{9,5},{10,... | collective-permute-start | bytes 786440 | tf_op jit(solution)/shard_map/ppermute | solution.py:78
  11.9 6.6 %collective-permute-done.4.refs_1_ = f32[128,512]{1,0:T(8,128)S(1)} collective-permute-done((f32[128,512]{1,0:T(8,128)S(1)}, f32[128,512]{1,0:T(8,128)S(1)}, u32[]{:S(2)}, u32[]{:S(2)}) %collective-permute-start.4) | collective-permute-done | bytes 262176 | tf_op jit(solution)/shard_map/ppermute | solution.py:78
  18.5 1.9 %collective-permute-start.11 = (f32[128,512]{1,0:T(8,128)S(1)}, f32[128,512]{1,0:T(8,128)S(1)}, u32[]{:S(2)}, u32[]{:S(2)}) collective-permute-start(f32[128,512]{1,0:T(8,128)S(1)} %multiply_subtract_fusion.refs_0_), channel_id=1, source_target_pairs={{0,3},{1,0},{2,1},{3,2},{4,7},{5,4},{6,5},{7,6},{8,11},{9,8},{10,9... | collective-permute-start | bytes 786440 | tf_op jit(solution)/shard_map/ppermute | solution.py:59
  20.4 2.3 %collective-permute-done.1.refs_5_ = f32[128,512]{1,0:T(8,128)S(1)} collective-permute-done((f32[128,512]{1,0:T(8,128)S(1)}, f32[128,512]{1,0:T(8,128)S(1)}, u32[]{:S(2)}, u32[]{:S(2)}) %collective-permute-start.1) | collective-permute-done | bytes 262176 | tf_op jit(solution)/shard_map/ppermute | solution.py:78
  22.7 3.2 %collective-permute-start.10 = (f32[128,512]{1,0:T(8,128)S(1)}, f32[128,512]{1,0:T(8,128)S(1)}, u32[]{:S(2)}, u32[]{:S(2)}) collective-permute-start(f32[128,512]{1,0:T(8,128)S(1)} %collective-permute-done.9.refs_6_), channel_id=1, source_target_pairs={{0,4},{1,5},{2,6},{3,7},{4,0},{5,1},{6,2},{7,3},{8,12},{9,13},{10,... | collective-permute-start | bytes 786440 | tf_op jit(solution)/shard_map/ppermute | solution.py:78
  25.9 2.3 %collective-permute-start.6 = (f32[128,512]{1,0:T(8,128)S(1)}, f32[128,512]{1,0:T(8,128)S(1)}, u32[]{:S(2)}, u32[]{:S(2)}) collective-permute-start(f32[128,512]{1,0:T(8,128)S(1)} %collective-permute-done.5.refs_2_), channel_id=1, source_target_pairs={{0,4},{1,5},{2,6},{3,7},{4,0},{5,1},{6,2},{7,3},{8,12},{9,13},{10,... | collective-permute-start | bytes 786440 | tf_op jit(solution)/shard_map/ppermute | solution.py:78
  28.2 5.6 %collective-permute-start.8 = (f32[128,512]{1,0:T(8,128)S(1)}, f32[128,512]{1,0:T(8,128)S(1)}, u32[]{:S(2)}, u32[]{:S(2)}) collective-permute-start(f32[128,512]{1,0:T(8,128)S(1)} %collective-permute-done.7.refs_4_), channel_id=1, source_target_pairs={{0,4},{1,5},{2,6},{3,7},{4,0},{5,1},{6,2},{7,3},{8,12},{9,13},{10,... | collective-permute-start | bytes 786440 | tf_op jit(solution)/shard_map/ppermute | solution.py:78
  33.8 3.2 %collective-permute-start.3 = (f32[128,512]{1,0:T(8,128)S(1)}, f32[128,512]{1,0:T(8,128)S(1)}, u32[]{:S(2)}, u32[]{:S(2)}) collective-permute-start(f32[128,512]{1,0:T(8,128)S(1)} %collective-permute-done.2.refs_0_), channel_id=1, source_target_pairs={{0,4},{1,5},{2,6},{3,7},{4,0},{5,1},{6,2},{7,3},{8,12},{9,13},{10,... | collective-permute-start | bytes 786440 | tf_op jit(solution)/shard_map/ppermute | solution.py:78
  37.0 1.6 %collective-permute-done.6.refs_3_ = f32[128,512]{1,0:T(8,128)S(1)} collective-permute-done((f32[128,512]{1,0:T(8,128)S(1)}, f32[128,512]{1,0:T(8,128)S(1)}, u32[]{:S(2)}, u32[]{:S(2)}) %collective-permute-start.6) | collective-permute-done | bytes 262176 | tf_op jit(solution)/shard_map/ppermute | solution.py:78
  38.6 1.8 %shard_map.147 = (f32[384,512]{1,0:T(8,128)S(1)}, f32[384,384]{1,0:T(8,128)S(1)}, f32[128,512]{1,0:T(8,128)S(1)}, f32[128,512]{1,0:T(8,128)S(1)}) custom-call(f32[128,512]{1,0:T(8,128)S(1)} %multiply_subtract_fusion.refs_0_, f32[128,512]{1,0:T(8,128)S(1)} %collective-permute-done.4.refs_1_, f32[128,512]{1,0:T(8,128)S(1)} %collective-permute-done.5.refs_2_, ...), custom_call_target="tpu_custom_call" | custom-call | flops 1207959552 | bytes 6359552 | tf_op jit(solution)/shard_map/pallas_call | solution.py:126
  40.4 3.8 %collective-permute-done.8.refs_5_ = f32[128,512]{1,0:T(8,128)S(1)} collective-permute-done((f32[128,512]{1,0:T(8,128)S(1)}, f32[128,512]{1,0:T(8,128)S(1)}, u32[]{:S(2)}, u32[]{:S(2)}) %collective-permute-start.8) | collective-permute-done | bytes 262176 | tf_op jit(solution)/shard_map/ppermute | solution.py:78
  44.3 3.9 %shard_map.148 = (f32[512,512]{1,0:T(8,128)S(1)}, f32[1,512]{1,0:T(1,128)S(1)}, bf16[512,128]{1,0:T(8,128)(2,1)S(1)}, bf16[512,128]{1,0:T(8,128)(2,1)S(1)}, f32[...) custom-call(f32[128,512]{1,0:T(8,128)S(1)} %multiply_subtract_fusion.refs_0_, ...), custom_call_target="tpu_custom_call" | custom-call | flops 2617245696 | bytes 5705728 | tf_op jit(solution)/shard_map/pallas_call | solution.py:126
  48.2 0.1 collective-permute-done.3.refs_1_
  48.3 1.7 %shard_map.149 = (f32[1,128,512]{2,1,0:T(8,128)}, f32[1,128,512]{2,1,0:T(8,128)}, f32[1,128,512]{2,1,0:T(8,128)}, f32[1,512,512]{2,1,0:T(8,128)}, f32[1,512]{1,0:T(1,128)}) custom-call(f32[128,512]{1,0:T(8,128)S(1)} %collective-permute-done.2.refs_0_, f32[128,512]{1,0:T(8,128)S(1)} %collective-permute-done.3.refs_1_, ...), custom_call_target="tpu_custom_call" | custom-call | flops 402653184 | bytes 4591616 | tf_op jit(solution)/shard_map/pallas_call | solution.py:126
  (22 shorter events, 0.1 us)
Async XLA Ops:
  0.6 2.2 %copy-start = (f32[128,512]{1,0:T(8,128)S(1)}, f32[128,512]{1,0:T(8,128)}, u32[]{:S(2)}) copy-start(f32[128,512]{1,0:T(8,128)} %qb.1) | copy-start | bytes 786436
  0.6 2.2 %copy-start.1 = (f32[128,512]{1,0:T(8,128)S(1)}, f32[128,512]{1,0:T(8,128)}, u32[]{:S(2)}) copy-start(f32[128,512]{1,0:T(8,128)} %ub.1) | copy-start | bytes 786436
  2.3 6.5 %collective-permute-start = (f32[128,512]{1,0:T(8,128)S(1)}, f32[128,512]{1,0:T(8,128)S(1)}, u32[]{:S(2)}, u32[]{:S(2)}) collective-permute-start(f32[128,512]{1,0:T(8,128)S(1)} %get-tuple-element.31), channel_id=1, source_target_pairs={{0,1},{1,2},{2,3},{3,0},{4,5},{5,6},{6,7},{7,4},{8,9},{9,10},{10,1... | collective-permute-start | bytes 786440 | tf_op jit(solution)/shard_map/ppermute | solution.py:59
  2.8 0.7 %copy-start.5 = (s32[1,128]{1,0:T(1,128)S(1)}, s32[1,128]{1,0:T(1,128)}, u32[]{:S(2)}) copy-start(s32[1,128]{1,0:T(1,128)} %refs_15_.1) | copy-start | bytes 1540
  3.5 7.8 %copy-start.7 = (f32[1,128,512]{2,1,0:T(8,128)S(1)}, f32[1,128,512]{2,1,0:T(8,128)}, u32[]{:S(2)}) copy-start(f32[1,128,512]{2,1,0:T(8,128)} %refs_3_.1) | copy-start | bytes 786436
  4.8 33.9 %copy-start.2 = (f32[1,128,512]{2,1,0:T(8,128)S(1)}, f32[1,128,512]{2,1,0:T(8,128)}, u32[]{:S(2)}) copy-start(f32[1,128,512]{2,1,0:T(8,128)} %refs_12_.1) | copy-start | bytes 786436
  4.8 33.9 %copy-start.3 = (f32[1,128,512]{2,1,0:T(8,128)S(1)}, f32[1,128,512]{2,1,0:T(8,128)}, u32[]{:S(2)}) copy-start(f32[1,128,512]{2,1,0:T(8,128)} %refs_11_.1) | copy-start | bytes 786436
  4.8 33.9 %copy-start.6 = (f32[128,512]{1,0:T(8,128)S(1)}, f32[128,512]{1,0:T(8,128)}, u32[]{:S(2)}) copy-start(f32[128,512]{1,0:T(8,128)} %refs_14_.1) | copy-start | bytes 786436
  8.9 35.4 %copy-start.4 = (f32[128,512]{1,0:T(8,128)}, f32[128,512]{1,0:T(8,128)S(1)}, u32[]{:S(2)}) copy-start(f32[128,512]{1,0:T(8,128)S(1)} %multiply_subtract_fusion.refs_0_) | copy-start | bytes 786436
  8.9 9.6 %collective-permute-start.4 = (f32[128,512]{1,0:T(8,128)S(1)}, f32[128,512]{1,0:T(8,128)S(1)}, u32[]{:S(2)}, u32[]{:S(2)}) collective-permute-start(f32[128,512]{1,0:T(8,128)S(1)} %multiply_subtract_fusion.refs_0_), channel_id=1, source_target_pairs={{0,4},{1,5},{2,6},{3,7},{4,0},{5,1},{6,2},{7,3},{8,12},{9,13},{10,... | collective-permute-start | bytes 786440 | tf_op jit(solution)/shard_map/ppermute | solution.py:78
  11.3 11.4 %collective-permute-start.1 = (f32[128,512]{1,0:T(8,128)S(1)}, f32[128,512]{1,0:T(8,128)S(1)}, u32[]{:S(2)}, u32[]{:S(2)}) collective-permute-start(f32[128,512]{1,0:T(8,128)S(1)} %bitcast.5), channel_id=1, source_target_pairs={{0,4},{1,5},{2,6},{3,7},{4,0},{5,1},{6,2},{7,3},{8,12},{9,13},{10,... | collective-permute-start | bytes 786440 | tf_op jit(solution)/shard_map/ppermute | solution.py:78
  11.4 11.3 %collective-permute-start.9 = (f32[128,512]{1,0:T(8,128)S(1)}, f32[128,512]{1,0:T(8,128)S(1)}, u32[]{:S(2)}, u32[]{:S(2)}) collective-permute-start(f32[128,512]{1,0:T(8,128)S(1)} %bitcast.6), channel_id=1, source_target_pairs={{0,1},{1,0},{2,3},{3,2},{4,8},{5,9},{6,10},{7,11},{8,4},{9,5},{10,... | collective-permute-start | bytes 786440 | tf_op jit(solution)/shard_map/ppermute | solution.py:78
  11.4 14.4 %collective-permute-start.5 = (f32[128,512]{1,0:T(8,128)S(1)}, f32[128,512]{1,0:T(8,128)S(1)}, u32[]{:S(2)}, u32[]{:S(2)}) collective-permute-start(f32[128,512]{1,0:T(8,128)S(1)} %multiply_subtract_fusion.refs_0_), channel_id=1, source_target_pairs={{0,1},{1,0},{2,3},{3,2},{4,8},{5,9},{6,10},{7,11},{8,4},{9,5},{10,... | collective-permute-start | bytes 786440 | tf_op jit(solution)/shard_map/ppermute | solution.py:78
  18.5 9.7 %collective-permute-start.7 = (f32[128,512]{1,0:T(8,128)S(1)}, f32[128,512]{1,0:T(8,128)S(1)}, u32[]{:S(2)}, u32[]{:S(2)}) collective-permute-start(f32[128,512]{1,0:T(8,128)S(1)} %collective-permute-done.4.refs_1_), channel_id=1, source_target_pairs={{0,1},{1,0},{2,3},{3,2},{4,8},{5,9},{6,10},{7,11},{8,4},{9,5},{10,... | collective-permute-start | bytes 786440 | tf_op jit(solution)/shard_map/ppermute | solution.py:78
  18.5 18.5 %collective-permute-start.11 = (f32[128,512]{1,0:T(8,128)S(1)}, f32[128,512]{1,0:T(8,128)S(1)}, u32[]{:S(2)}, u32[]{:S(2)}) collective-permute-start(f32[128,512]{1,0:T(8,128)S(1)} %multiply_subtract_fusion.refs_0_), channel_id=1, source_target_pairs={{0,3},{1,0},{2,1},{3,2},{4,7},{5,4},{6,5},{7,6},{8,11},{9,8},{10,9... | collective-permute-start | bytes 786440 | tf_op jit(solution)/shard_map/ppermute | solution.py:59
  22.7 11.1 %collective-permute-start.2 = (f32[128,512]{1,0:T(8,128)S(1)}, f32[128,512]{1,0:T(8,128)S(1)}, u32[]{:S(2)}, u32[]{:S(2)}) collective-permute-start(f32[128,512]{1,0:T(8,128)S(1)} %collective-permute-done.1.refs_5_), channel_id=1, source_target_pairs={{0,1},{1,0},{2,3},{3,2},{4,8},{5,9},{6,10},{7,11},{8,4},{9,5},{10,... | collective-permute-start | bytes 786440 | tf_op jit(solution)/shard_map/ppermute | solution.py:78
  22.7 14.3 %collective-permute-start.10 = (f32[128,512]{1,0:T(8,128)S(1)}, f32[128,512]{1,0:T(8,128)S(1)}, u32[]{:S(2)}, u32[]{:S(2)}) collective-permute-start(f32[128,512]{1,0:T(8,128)S(1)} %collective-permute-done.9.refs_6_), channel_id=1, source_target_pairs={{0,4},{1,5},{2,6},{3,7},{4,0},{5,1},{6,2},{7,3},{8,12},{9,13},{10,... | collective-permute-start | bytes 786440 | tf_op jit(solution)/shard_map/ppermute | solution.py:78
  25.9 12.8 %collective-permute-start.6 = (f32[128,512]{1,0:T(8,128)S(1)}, f32[128,512]{1,0:T(8,128)S(1)}, u32[]{:S(2)}, u32[]{:S(2)}) collective-permute-start(f32[128,512]{1,0:T(8,128)S(1)} %collective-permute-done.5.refs_2_), channel_id=1, source_target_pairs={{0,4},{1,5},{2,6},{3,7},{4,0},{5,1},{6,2},{7,3},{8,12},{9,13},{10,... | collective-permute-start | bytes 786440 | tf_op jit(solution)/shard_map/ppermute | solution.py:78
  28.2 16.1 %collective-permute-start.8 = (f32[128,512]{1,0:T(8,128)S(1)}, f32[128,512]{1,0:T(8,128)S(1)}, u32[]{:S(2)}, u32[]{:S(2)}) collective-permute-start(f32[128,512]{1,0:T(8,128)S(1)} %collective-permute-done.7.refs_4_), channel_id=1, source_target_pairs={{0,4},{1,5},{2,6},{3,7},{4,0},{5,1},{6,2},{7,3},{8,12},{9,13},{10,... | collective-permute-start | bytes 786440 | tf_op jit(solution)/shard_map/ppermute | solution.py:78
  33.8 14.5 %collective-permute-start.3 = (f32[128,512]{1,0:T(8,128)S(1)}, f32[128,512]{1,0:T(8,128)S(1)}, u32[]{:S(2)}, u32[]{:S(2)}) collective-permute-start(f32[128,512]{1,0:T(8,128)S(1)} %collective-permute-done.2.refs_0_), channel_id=1, source_target_pairs={{0,4},{1,5},{2,6},{3,7},{4,0},{5,1},{6,2},{7,3},{8,12},{9,13},{10,... | collective-permute-start | bytes 786440 | tf_op jit(solution)/shard_map/ppermute | solution.py:78

commit v3 on v2

--- a/solution.py
+++ b/solution.py
@@ -222,12 +222,14 @@
     def early_kernel(*refs):
         ins = refs[: 2 * sum(sizes)]
         w, b, z, q, u, pn, pb, order = refs[2 * sum(sizes) : 2 * sum(sizes) + 8]
-        residual, kernel, z_part, q_part = refs[2 * sum(sizes) + 8 :]
+        residual, kernel, square, turned, z_part, q_part = refs[2 * sum(sizes) + 8 :]
         p_refs, z_refs = group(ins[: sum(sizes)], sizes), group(ins[sum(sizes) :], sizes)
         wide = split(w[0])
-        blocks = [split(block_of(r, m)) for r, m in zip(p_refs, members)]
+        whole = [block_of(r, m) for r, m in zip(p_refs, members)]
+        blocks = [split(block) for block in whole]
         for i, block in enumerate(blocks):
             at = slice(i * rows, (i + 1) * rows)
+            turned[:, at] = whole[i].T
             residual[at] = dot3(block, wide) + b[...] - block_of(z_refs[i], members[i])
             for j in range(i + 1):
                 to = slice(j * rows, (j + 1) * rows)
@@ -235,6 +237,8 @@
                 kernel[at, to] = piece
                 if j < i:
                     kernel[to, at] = piece.T
+        both = split(kernel[...])
+        square[...] = dot3(both, both)
         value = z[0]
         z_part[...] = (1 - step_preact) * value - step_preact * (
             (softplus(value) - q[0]) * jax.nn.sigmoid(value)
@@ -245,39 +249,47 @@
 
     args = [x for parts in p_early for x in parts] + [x for parts in z_early for x in parts]
     args += [weight, offset, preact, outputs, duals, after_in, next_inputs, row_order]
-    residual, kernel, z_part, q_part = run(
+    residual, kernel, square, turned, z_part, q_part = run(
         early_kernel,
         args,
-        [f32(early_count, width), f32(early_count, early_count), f32(rows, width), f32(rows, width)],
-        unit * (2 * len(sizes)),
+        [
+            f32(early_count, width),
+            f32(early_count, early_count),
+            f32(early_count, early_count),
+            f32(width, early_count),
+            f32(rows, width),
+            f32(rows, width),
+        ],
+        unit * (3 * len(sizes)),
     )
 
     def solve_kernel(*refs):
         ins = refs[: sum(sizes) + len(p_late)]
-        residual, kernel, w, b = refs[len(ins) : len(ins) + 4]
-        w_part, b_part, pull_high, pull_low, weigh, a_part, a_pull = refs[len(ins) + 4 : len(ins) + 11]
-        j_ref, turned = refs[len(ins) + 11 :]
+        residual, kernel, square, turned, w, b = refs[len(ins) : len(ins) + 6]
+        w_part, b_part, pull_high, pull_low, weigh, a_part, a_pull = refs[len(ins) + 6 : len(ins) + 13]
+        total_ref, turned_ref = refs[len(ins) + 13 :]
         wide = split(w[0])
         every = [block_of(r, m) for r, m in zip(group(ins, sizes + [len(p_late)]), members)]
         late = split(every[-1])
-        j_ref[:early_count, :early_count] = kernel[...]
-        for i, block in enumerate(every):
-            at = slice(i * rows, (i + 1) * rows)
-            turned[:, at] = block.T
-            piece = scale * (dot3(split(block), late, NT) + 1.0)
-            j_ref[at, early_count:] = piece
-            if i * rows < early_count:
-                j_ref[early_count:, at] = piece.T
-        j = j_ref[...]
-        both = split(j)
+        turned_ref[:, :early_count] = turned[...]
+        turned_ref[:, early_count:] = every[-1].T
+        edge = jnp.concatenate([scale * (dot3(split(x), late, NT) + 1.0) for x in every[:-1]], axis=0)
+        corner = scale * (dot3(late, late, NT) + 1.0)
+        edge_across, near = edge.T, kernel[...]
+        edge_split, across_split, corner_split = split(edge), split(edge_across), split(corner)
+        mixed = dot3(split(near), edge_split) + dot3(edge_split, corner_split) - INNER * edge
+        total_ref[:early_count, :early_count] = square[...] + dot3(edge_split, across_split) - INNER * near
+        total_ref[:early_count, early_count:] = mixed
+        total_ref[early_count:, :early_count] = mixed.T
+        total_ref[early_count:, early_count:] = (
+            dot3(across_split, edge_split) + dot3(corner_split, corner_split) - INNER * corner
+        )
         eye = (
             lax.broadcasted_iota(jnp.int32, (count, count), 0)
             == lax.broadcasted_iota(jnp.int32, (count, count), 1)
         ).astype(jnp.float32)
-        total = eye
-        for inner_step in range(1, INNER):
-            total = eye + total - (dot3(both, split(total)) if inner_step > 1 else j)
-        pull = scale * dot3(split(turned[...]), split(total))
+        total = total_ref[...] + INNER * eye
+        pull = scale * dot3(split(turned_ref[...]), split(total))
         sums = scale * jnp.sum(total, axis=1, keepdims=True)
         start = jnp.concatenate([residual[...], dot3(late, wide) + b[...]], axis=0)
         new = w[0] - dot3(split(pull), split(start))
@@ -290,7 +302,7 @@
         a_part[...] = dot3(own, split(new)) + new_b
         a_pull[...] = dot3(own, (pull_high[...], pull_low[...]))
 
-    args = [x for parts in p_early + [p_late] for x in parts] + [residual, kernel, weight, offset]
+    args = [x for parts in p_early + [p_late] for x in parts] + [residual, kernel, square, turned, weight, offset]
     solved = run(
         solve_kernel,
         args,
@@ -325,9 +337,6 @@
             copies.append(pltpu.make_async_copy(own.at[0, at], out.at[0, at], sems.at[len(copies)]))
             copies[-1].start()
 
-        for at in w_chunks:
-            w_own[0, at] = w_part[at] + dot3((pull_high[at], pull_low[at]), late)
-            send(w_own, w_out, at)
         shift = jnp.sum(weigh[:, :1] * value, axis=0, keepdims=True)
         b_own[...] = b_part[...] + shift
         copies.append(pltpu.make_async_copy(b_own, b_out, sems.at[len(copies)]))
@@ -343,6 +352,9 @@
             send(q_own, q_out, at)
             u_own[0, at] = both - penalty_rho * new_q
             send(u_own, u_out, at)
+        for at in w_chunks:
+            w_own[0, at] = w_part[at] + dot3((pull_high[at], pull_low[at]), late)
+            send(w_own, w_out, at)
         for copy in copies:
             copy.wait()
 
@@ -446,7 +458,7 @@
 def body(*args):
     inputs = args[0]
     count = lax.axis_size("dp")
-    gathers = 1 < count and inputs.shape[1] * count <= 2 * inputs.shape[2]
+    gathers = INNER == 3 and 1 < count and inputs.shape[1] * count <= 2 * inputs.shape[2]
     return (gathered_body if gathers else summed_body)(*args)
 
 

time: 50.1 us -> 51.2 us (1.022)
  Pallas kernels: 10.2 us -> 12.1 us
  waiting for transfers between devices: 18.5 us -> 17.7 us
    pallas_call x5, Pallas kernels: 10.2 us -> 12.1 us  [run(): pl.pallas_call(kernel, out_shape=outs, in_specs=[VMEM] * len(args) if in_...]
    ppermute x10, waiting for transfers between devices: 14.5 us -> 13.7 us  [gather_line(): arrived = lax.ppermute(payload, ('dp', 'layer'), whole_swap(swaps))]
  transfers between devices with their start and end apart: 12 -> 12, of which waited for: 6 -> 5; matrix products, arithmetic and copies ran while one was open for 0% -> 0% of each run, Pallas kernels for 14% -> 17%
where the time goes in v3:
time: 51.2 us; the launch traced here: 51.1 us
  starting transfers between devices  19.8 us (39%)
  waiting for transfers between devices  17.7 us (35%)
  Pallas kernels  12.1 us (24%)
  between operations  0.74 us (1%)
  local copies, waits for them, and re-layouts  0.69 us (1%)
    ppermute x10, starting transfers between devices, gather_line(): arrived = lax.ppermute(payload, ('dp', 'layer'), whole_swap(swaps))  17.3 us
    ppermute x10, waiting for transfers between devices, gather_line(): arrived = lax.ppermute(payload, ('dp', 'layer'), whole_swap(swaps))  13.7 us
    pallas_call x5, Pallas kernels, run(): pl.pallas_call(kernel, out_shape=outs, in_specs=[VMEM] * len(args) if in_...  12.1 us
    ppermute x2, waiting for transfers between devices, around(): lax.ppermute(x, 'layer', [(i, (i + by) % count) for i in range(count)])  4.01 us
    ppermute x2, starting transfers between devices, around(): lax.ppermute(x, 'layer', [(i, (i + by) % count) for i in range(count)])  2.44 us
  transfers between devices with their start and end apart: 12, of which 5 were waited for; matrix products, arithmetic and copies ran while one was open for 0% of the time, Pallas kernels for 17%

profile of v3, /device:TPU:0, one launch (start us, length us, event | category | flops | bytes accessed | tf_op | source)
XLA Modules:
  0.0 51.1 jit_solution(4806652375091633752)
XLA Ops:
  0.7 1.6 %shard_map.145 = (f32[128,512]{1,0:T(8,128)S(1)}, f32[1,128,512]{2,1,0:T(8,128)S(1)}, f32[1,512,512]{2,1,0:T(8,128)S(1)}, f32[1,512]{1,0:T(1,128)S(1)}, f32[1,128,512]{2,1,0:T(8,128)S(1)}) custom-call(f32[1,128,512]{2,1,0:T(8,128)} %refs_12_.1, f32[1,128,512]{2,1,0:T(8,128)} %refs_11_.1, f32[1,128,512]{2,1,0:T(8,128)} %refs_0_.1, f32[1,512,512]{2,1,0:T(8,128)} %refs_1_.1, ...), custom_call_target="tpu_custom_call" | custom-call | flops 20132660 | bytes 3936256 | tf_op jit(solution)/shard_map/pallas_call | solution.py:126
  2.3 0.5 %collective-permute-start = (f32[128,512]{1,0:T(8,128)S(1)}, f32[128,512]{1,0:T(8,128)S(1)}, u32[]{:S(2)}, u32[]{:S(2)}) collective-permute-start(f32[128,512]{1,0:T(8,128)S(1)} %get-tuple-element.33), channel_id=1, source_target_pairs={{0,1},{1,2},{2,3},{3,0},{4,5},{5,6},{6,7},{7,4},{8,9},{9,10},{10,1... | collective-permute-start | bytes 786440 | tf_op jit(solution)/shard_map/ppermute | solution.py:59
  2.8 0.6 %copy-done.5 = s32[1,128]{1,0:T(1,128)S(1)} copy-done((s32[1,128]{1,0:T(1,128)S(1)}, s32[1,128]{1,0:T(1,128)}, u32[]{:S(2)}) %copy-start.5) | copy-done | bytes 536
  3.5 1.3 %shard_map.146 = f32[128,512]{1,0:T(8,128)S(1)} custom-call(f32[1,128,512]{2,1,0:T(8,128)S(1)} %get-tuple-element.29.p, f32[1,512,512]{2,1,0:T(8,128)S(1)} %get-tuple-element.30.w.refs_8_.refs_10_, f32[1,512]{1,0:T(1,128)S(1)} %get-tuple-element.31.b.refs_9_.refs_11_, f32[1,128,512]{2,1,0:T(8,128)S(1)} %get-tuple-element.32.z.refs_10_, ...), custom_call_target="tpu_custom_call" | custom-call | flops 402653184 | bytes 2361856 | tf_op jit(solution)/shard_map/pallas_call | solution.py:126
  4.8 0.0 copy-start.2
  4.8 0.0 copy-start.3
  4.8 0.0 copy-start.6
  4.8 4.0 %collective-permute-done = f32[128,512]{1,0:T(8,128)S(1)} collective-permute-done((f32[128,512]{1,0:T(8,128)S(1)}, f32[128,512]{1,0:T(8,128)S(1)}, u32[]{:S(2)}, u32[]{:S(2)}) %collective-permute-start) | collective-permute-done | bytes 262176 | tf_op jit(solution)/shard_map/ppermute | solution.py:59
  8.9 0.0 copy-start.4
  8.9 2.5 %collective-permute-start.4 = (f32[128,512]{1,0:T(8,128)S(1)}, f32[128,512]{1,0:T(8,128)S(1)}, u32[]{:S(2)}, u32[]{:S(2)}) collective-permute-start(f32[128,512]{1,0:T(8,128)S(1)} %multiply_subtract_fusion.refs_0_), channel_id=1, source_target_pairs={{0,4},{1,5},{2,6},{3,7},{4,0},{5,1},{6,2},{7,3},{8,12},{9,13},{10,... | collective-permute-start | bytes 786440 | tf_op jit(solution)/shard_map/ppermute | solution.py:78
  11.3 0.1 collective-permute-start.1
  11.4 0.5 collective-permute-start.5
  11.9 6.6 %collective-permute-done.4.refs_1_ = f32[128,512]{1,0:T(8,128)S(1)} collective-permute-done((f32[128,512]{1,0:T(8,128)S(1)}, f32[128,512]{1,0:T(8,128)S(1)}, u32[]{:S(2)}, u32[]{:S(2)}) %collective-permute-start.4) | collective-permute-done | bytes 262176 | tf_op jit(solution)/shard_map/ppermute | solution.py:78
  18.5 1.9 %collective-permute-start.11 = (f32[128,512]{1,0:T(8,128)S(1)}, f32[128,512]{1,0:T(8,128)S(1)}, u32[]{:S(2)}, u32[]{:S(2)}) collective-permute-start(f32[128,512]{1,0:T(8,128)S(1)} %multiply_subtract_fusion.refs_0_), channel_id=1, source_target_pairs={{0,3},{1,0},{2,1},{3,2},{4,7},{5,4},{6,5},{7,6},{8,11},{9,8},{10,9... | collective-permute-start | bytes 786440 | tf_op jit(solution)/shard_map/ppermute | solution.py:59
  20.4 2.3 %collective-permute-done.1.refs_5_ = f32[128,512]{1,0:T(8,128)S(1)} collective-permute-done((f32[128,512]{1,0:T(8,128)S(1)}, f32[128,512]{1,0:T(8,128)S(1)}, u32[]{:S(2)}, u32[]{:S(2)}) %collective-permute-start.1) | collective-permute-done | bytes 262176 | tf_op jit(solution)/shard_map/ppermute | solution.py:78
  22.7 3.2 %collective-permute-start.10 = (f32[128,512]{1,0:T(8,128)S(1)}, f32[128,512]{1,0:T(8,128)S(1)}, u32[]{:S(2)}, u32[]{:S(2)}) collective-permute-start(f32[128,512]{1,0:T(8,128)S(1)} %collective-permute-done.9.refs_6_), channel_id=1, source_target_pairs={{0,4},{1,5},{2,6},{3,7},{4,0},{5,1},{6,2},{7,3},{8,12},{9,13},{10,... | collective-permute-start | bytes 786440 | tf_op jit(solution)/shard_map/ppermute | solution.py:78
  25.9 2.3 %collective-permute-start.6 = (f32[128,512]{1,0:T(8,128)S(1)}, f32[128,512]{1,0:T(8,128)S(1)}, u32[]{:S(2)}, u32[]{:S(2)}) collective-permute-start(f32[128,512]{1,0:T(8,128)S(1)} %collective-permute-done.5.refs_2_), channel_id=1, source_target_pairs={{0,4},{1,5},{2,6},{3,7},{4,0},{5,1},{6,2},{7,3},{8,12},{9,13},{10,... | collective-permute-start | bytes 786440 | tf_op jit(solution)/shard_map/ppermute | solution.py:78
  28.2 5.6 %collective-permute-start.8 = (f32[128,512]{1,0:T(8,128)S(1)}, f32[128,512]{1,0:T(8,128)S(1)}, u32[]{:S(2)}, u32[]{:S(2)}) collective-permute-start(f32[128,512]{1,0:T(8,128)S(1)} %collective-permute-done.7.refs_4_), channel_id=1, source_target_pairs={{0,4},{1,5},{2,6},{3,7},{4,0},{5,1},{6,2},{7,3},{8,12},{9,13},{10,... | collective-permute-start | bytes 786440 | tf_op jit(solution)/shard_map/ppermute | solution.py:78
  33.8 3.2 %collective-permute-start.3 = (f32[128,512]{1,0:T(8,128)S(1)}, f32[128,512]{1,0:T(8,128)S(1)}, u32[]{:S(2)}, u32[]{:S(2)}) collective-permute-start(f32[128,512]{1,0:T(8,128)S(1)} %collective-permute-done.2.refs_0_), channel_id=1, source_target_pairs={{0,4},{1,5},{2,6},{3,7},{4,0},{5,1},{6,2},{7,3},{8,12},{9,13},{10,... | collective-permute-start | bytes 786440 | tf_op jit(solution)/shard_map/ppermute | solution.py:78
  37.0 1.6 %collective-permute-done.6.refs_3_ = f32[128,512]{1,0:T(8,128)S(1)} collective-permute-done((f32[128,512]{1,0:T(8,128)S(1)}, f32[128,512]{1,0:T(8,128)S(1)}, u32[]{:S(2)}, u32[]{:S(2)}) %collective-permute-start.6) | collective-permute-done | bytes 262176 | tf_op jit(solution)/shard_map/ppermute | solution.py:78
  38.6 2.4 %shard_map.147 = (f32[384,512]{1,0:T(8,128)S(1)}, f32[384,384]{1,0:T(8,128)S(1)}, f32[384,384]{1,0:T(8,128)S(1)}, f32[512,384]{1,0:T(8,128)S(1)}, f32[128,512]{1,0:T(8,128)S(1)}, /*index=5*/f32[128,512]{1,0:T(8,128)S(1)}) custom-call(f32[128,512]{1,0:T(8,128)S(1)} %multiply_subtract_fusion.refs_0_, f32[128,512]{1,0:T(8,128)S(1)} %collective-permute-done.4.refs_1_, ...), custom_call_target="tpu_custom_call" | custom-call | flops 1811939328 | bytes 7735808 | tf_op jit(solution)/shard_map/pallas_call | solution.py:126
  41.1 3.2 %collective-permute-done.8.refs_5_ = f32[128,512]{1,0:T(8,128)S(1)} collective-permute-done((f32[128,512]{1,0:T(8,128)S(1)}, f32[128,512]{1,0:T(8,128)S(1)}, u32[]{:S(2)}, u32[]{:S(2)}) %collective-permute-start.8) | collective-permute-done | bytes 262176 | tf_op jit(solution)/shard_map/ppermute | solution.py:78
  44.3 5.2 %shard_map.148 = (f32[512,512]{1,0:T(8,128)S(1)}, f32[1,512]{1,0:T(1,128)S(1)}, bf16[512,128]{1,0:T(8,128)(2,1)S(1)}, bf16[512,128]{1,0:T(8,128)(2,1)S(1)}, f32[...) custom-call(f32[128,512]{1,0:T(8,128)S(1)} %multiply_subtract_fusion.refs_0_, ...), custom_call_target="tpu_custom_call" | custom-call | flops 2617245696 | bytes 7081984 | tf_op jit(solution)/shard_map/pallas_call | solution.py:126
  49.4 1.6 %shard_map.149 = (f32[1,128,512]{2,1,0:T(8,128)}, f32[1,128,512]{2,1,0:T(8,128)}, f32[1,128,512]{2,1,0:T(8,128)}, f32[1,512,512]{2,1,0:T(8,128)}, f32[1,512]{1,0:T(1,128)}) custom-call(f32[128,512]{1,0:T(8,128)S(1)} %collective-permute-done.2.refs_0_, f32[128,512]{1,0:T(8,128)S(1)} %collective-permute-done.3.refs_1_, ...), custom_call_target="tpu_custom_call" | custom-call | flops 402653184 | bytes 4591616 | tf_op jit(solution)/shard_map/pallas_call | solution.py:126
  (22 shorter events, 0.1 us)
Async XLA Ops:
  0.6 2.2 %copy-start = (f32[128,512]{1,0:T(8,128)S(1)}, f32[128,512]{1,0:T(8,128)}, u32[]{:S(2)}) copy-start(f32[128,512]{1,0:T(8,128)} %qb.1) | copy-start | bytes 786436
  0.6 2.2 %copy-start.1 = (f32[128,512]{1,0:T(8,128)S(1)}, f32[128,512]{1,0:T(8,128)}, u32[]{:S(2)}) copy-start(f32[128,512]{1,0:T(8,128)} %ub.1) | copy-start | bytes 786436
  2.3 6.5 %collective-permute-start = (f32[128,512]{1,0:T(8,128)S(1)}, f32[128,512]{1,0:T(8,128)S(1)}, u32[]{:S(2)}, u32[]{:S(2)}) collective-permute-start(f32[128,512]{1,0:T(8,128)S(1)} %get-tuple-element.33), channel_id=1, source_target_pairs={{0,1},{1,2},{2,3},{3,0},{4,5},{5,6},{6,7},{7,4},{8,9},{9,10},{10,1... | collective-permute-start | bytes 786440 | tf_op jit(solution)/shard_map/ppermute | solution.py:59
  2.8 0.7 %copy-start.5 = (s32[1,128]{1,0:T(1,128)S(1)}, s32[1,128]{1,0:T(1,128)}, u32[]{:S(2)}) copy-start(s32[1,128]{1,0:T(1,128)} %refs_15_.1) | copy-start | bytes 1540
  3.5 7.8 %copy-start.7 = (f32[1,128,512]{2,1,0:T(8,128)S(1)}, f32[1,128,512]{2,1,0:T(8,128)}, u32[]{:S(2)}) copy-start(f32[1,128,512]{2,1,0:T(8,128)} %refs_3_.1) | copy-start | bytes 786436
  4.8 33.9 %copy-start.2 = (f32[1,128,512]{2,1,0:T(8,128)S(1)}, f32[1,128,512]{2,1,0:T(8,128)}, u32[]{:S(2)}) copy-start(f32[1,128,512]{2,1,0:T(8,128)} %refs_12_.1) | copy-start | bytes 786436
  4.8 33.9 %copy-start.3 = (f32[1,128,512]{2,1,0:T(8,128)S(1)}, f32[1,128,512]{2,1,0:T(8,128)}, u32[]{:S(2)}) copy-start(f32[1,128,512]{2,1,0:T(8,128)} %refs_11_.1) | copy-start | bytes 786436
  4.8 33.9 %copy-start.6 = (f32[128,512]{1,0:T(8,128)S(1)}, f32[128,512]{1,0:T(8,128)}, u32[]{:S(2)}) copy-start(f32[128,512]{1,0:T(8,128)} %refs_14_.1) | copy-start | bytes 786436
  8.9 35.4 %copy-start.4 = (f32[128,512]{1,0:T(8,128)}, f32[128,512]{1,0:T(8,128)S(1)}, u32[]{:S(2)}) copy-start(f32[128,512]{1,0:T(8,128)S(1)} %multiply_subtract_fusion.refs_0_) | copy-start | bytes 786436
  8.9 9.6 %collective-permute-start.4 = (f32[128,512]{1,0:T(8,128)S(1)}, f32[128,512]{1,0:T(8,128)S(1)}, u32[]{:S(2)}, u32[]{:S(2)}) collective-permute-start(f32[128,512]{1,0:T(8,128)S(1)} %multiply_subtract_fusion.refs_0_), channel_id=1, source_target_pairs={{0,4},{1,5},{2,6},{3,7},{4,0},{5,1},{6,2},{7,3},{8,12},{9,13},{10,... | collective-permute-start | bytes 786440 | tf_op jit(solution)/shard_map/ppermute | solution.py:78
  11.3 11.4 %collective-permute-start.1 = (f32[128,512]{1,0:T(8,128)S(1)}, f32[128,512]{1,0:T(8,128)S(1)}, u32[]{:S(2)}, u32[]{:S(2)}) collective-permute-start(f32[128,512]{1,0:T(8,128)S(1)} %bitcast.5), channel_id=1, source_target_pairs={{0,4},{1,5},{2,6},{3,7},{4,0},{5,1},{6,2},{7,3},{8,12},{9,13},{10,... | collective-permute-start | bytes 786440 | tf_op jit(solution)/shard_map/ppermute | solution.py:78
  11.4 11.3 %collective-permute-start.9 = (f32[128,512]{1,0:T(8,128)S(1)}, f32[128,512]{1,0:T(8,128)S(1)}, u32[]{:S(2)}, u32[]{:S(2)}) collective-permute-start(f32[128,512]{1,0:T(8,128)S(1)} %bitcast.6), channel_id=1, source_target_pairs={{0,1},{1,0},{2,3},{3,2},{4,8},{5,9},{6,10},{7,11},{8,4},{9,5},{10,... | collective-permute-start | bytes 786440 | tf_op jit(solution)/shard_map/ppermute | solution.py:78
  11.4 14.4 %collective-permute-start.5 = (f32[128,512]{1,0:T(8,128)S(1)}, f32[128,512]{1,0:T(8,128)S(1)}, u32[]{:S(2)}, u32[]{:S(2)}) collective-permute-start(f32[128,512]{1,0:T(8,128)S(1)} %multiply_subtract_fusion.refs_0_), channel_id=1, source_target_pairs={{0,1},{1,0},{2,3},{3,2},{4,8},{5,9},{6,10},{7,11},{8,4},{9,5},{10,... | collective-permute-start | bytes 786440 | tf_op jit(solution)/shard_map/ppermute | solution.py:78
  18.5 9.7 %collective-permute-start.7 = (f32[128,512]{1,0:T(8,128)S(1)}, f32[128,512]{1,0:T(8,128)S(1)}, u32[]{:S(2)}, u32[]{:S(2)}) collective-permute-start(f32[128,512]{1,0:T(8,128)S(1)} %collective-permute-done.4.refs_1_), channel_id=1, source_target_pairs={{0,1},{1,0},{2,3},{3,2},{4,8},{5,9},{6,10},{7,11},{8,4},{9,5},{10,... | collective-permute-start | bytes 786440 | tf_op jit(solution)/shard_map/ppermute | solution.py:78
  18.5 18.5 %collective-permute-start.11 = (f32[128,512]{1,0:T(8,128)S(1)}, f32[128,512]{1,0:T(8,128)S(1)}, u32[]{:S(2)}, u32[]{:S(2)}) collective-permute-start(f32[128,512]{1,0:T(8,128)S(1)} %multiply_subtract_fusion.refs_0_), channel_id=1, source_target_pairs={{0,3},{1,0},{2,1},{3,2},{4,7},{5,4},{6,5},{7,6},{8,11},{9,8},{10,9... | collective-permute-start | bytes 786440 | tf_op jit(solution)/shard_map/ppermute | solution.py:59
  22.7 11.1 %collective-permute-start.2 = (f32[128,512]{1,0:T(8,128)S(1)}, f32[128,512]{1,0:T(8,128)S(1)}, u32[]{:S(2)}, u32[]{:S(2)}) collective-permute-start(f32[128,512]{1,0:T(8,128)S(1)} %collective-permute-done.1.refs_5_), channel_id=1, source_target_pairs={{0,1},{1,0},{2,3},{3,2},{4,8},{5,9},{6,10},{7,11},{8,4},{9,5},{10,... | collective-permute-start | bytes 786440 | tf_op jit(solution)/shard_map/ppermute | solution.py:78
  22.7 14.3 %collective-permute-start.10 = (f32[128,512]{1,0:T(8,128)S(1)}, f32[128,512]{1,0:T(8,128)S(1)}, u32[]{:S(2)}, u32[]{:S(2)}) collective-permute-start(f32[128,512]{1,0:T(8,128)S(1)} %collective-permute-done.9.refs_6_), channel_id=1, source_target_pairs={{0,4},{1,5},{2,6},{3,7},{4,0},{5,1},{6,2},{7,3},{8,12},{9,13},{10,... | collective-permute-start | bytes 786440 | tf_op jit(solution)/shard_map/ppermute | solution.py:78
  25.9 12.8 %collective-permute-start.6 = (f32[128,512]{1,0:T(8,128)S(1)}, f32[128,512]{1,0:T(8,128)S(1)}, u32[]{:S(2)}, u32[]{:S(2)}) collective-permute-start(f32[128,512]{1,0:T(8,128)S(1)} %collective-permute-done.5.refs_2_), channel_id=1, source_target_pairs={{0,4},{1,5},{2,6},{3,7},{4,0},{5,1},{6,2},{7,3},{8,12},{9,13},{10,... | collective-permute-start | bytes 786440 | tf_op jit(solution)/shard_map/ppermute | solution.py:78
  28.2 16.1 %collective-permute-start.8 = (f32[128,512]{1,0:T(8,128)S(1)}, f32[128,512]{1,0:T(8,128)S(1)}, u32[]{:S(2)}, u32[]{:S(2)}) collective-permute-start(f32[128,512]{1,0:T(8,128)S(1)} %collective-permute-done.7.refs_4_), channel_id=1, source_target_pairs={{0,4},{1,5},{2,6},{3,7},{4,0},{5,1},{6,2},{7,3},{8,12},{9,13},{10,... | collective-permute-start | bytes 786440 | tf_op jit(solution)/shard_map/ppermute | solution.py:78
  33.8 15.7 %collective-permute-start.3 = (f32[128,512]{1,0:T(8,128)S(1)}, f32[128,512]{1,0:T(8,128)S(1)}, u32[]{:S(2)}, u32[]{:S(2)}) collective-permute-start(f32[128,512]{1,0:T(8,128)S(1)} %collective-permute-done.2.refs_0_), channel_id=1, source_target_pairs={{0,4},{1,5},{2,6},{3,7},{4,0},{5,1},{6,2},{7,3},{8,12},{9,13},{10,... | collective-permute-start | bytes 786440 | tf_op jit(solution)/shard_map/ppermute | solution.py:78
